TPU v7x, 32 devices: a whole 2x2x4 slice. The times are simulated.
32 devices in a mesh: dp: 8 (over z, x), tensor: 4 (over y, core).
Axes of the slice: x: 2, y: 2, z: 4, core: 2. Of those that a mesh axis runs over, the one named last changes fastest.
Arguments:
- residual: bfloat16 [2, 512, 5120], P(None, 'dp'), may hold values from -6 to 6
- context: bfloat16 [2, 512, 1536], P(None, 'dp', 'tensor'), may hold values from -6 to 6
- w_out: bfloat16 [1536, 5120], P('tensor'), may hold values from -0.15625 to 0.15625
- gain: float32 [5120], replicated, may hold values from 0.1 to 1.9
- cotangent: bfloat16 [2, 512, 5120], P(None, 'dp'), may hold values from -6 to 6
- slot_rows: int32 [4, 32], P('tensor'), may hold values from 0 to 383, as said below
Outputs:
- grad_slots: float32 [4, 5120, 32], P('tensor', 'dp')
- ctx_grad: bfloat16 [2, 512, 1536], P(None, 'dp', 'tensor')
- resid_grad: bfloat16 [2, 512, 5120], P(None, 'dp')
Inputs may be any that keep to these rules, and one draw needn't show every extreme that they name: Each row of slot_rows holds 32 different numbers.
All inputs are finite; a program needn't handle non-finite values.
Results may differ from a plain program's by a relative error of at most 0.006.
Values may be sent and summed in bfloat16 or wider, within the bound.
A program may use at most 64 MiB of HBM per device.

v0:
```python
import functools

import jax
import jax.numpy as jnp
from jax import lax
from jax.experimental import pallas as pl
from jax.experimental.pallas import tpu as pltpu
from jax.sharding import PartitionSpec as P

MESH = pl.DeviceIdType.MESH
ANY = pl.BlockSpec(memory_space=pl.ANY)
VMEM = pl.BlockSpec(memory_space=pltpu.VMEM)
F32 = jnp.float32
BF16 = jnp.bfloat16
LANES = 128
ROWS = 16
VMEM_BYTES = 67043328


def pieces_of(width):
    for count in (5, 4, 2):
        if width % (count * LANES) == 0:
            return count
    return 1


def norm_backward(hidden, cot_rows, gain):
    scale = 1.0 / hidden.shape[-1]
    center = hidden - jnp.sum(hidden, axis=-1, keepdims=True) * scale
    inverse = lax.rsqrt(jnp.sum(center * center, axis=-1, keepdims=True) * scale + 1e-05)
    upstream = cot_rows.astype(F32) * gain
    mean_up = jnp.sum(upstream, axis=-1, keepdims=True) * scale
    slope = jnp.sum(upstream * center, axis=-1, keepdims=True) * scale * inverse * inverse
    return (inverse * (upstream - mean_up - center * slope)).astype(BF16)


def kernel(reduce_dp, replicas, tensors, res_hbm, ctx_hbm, w_hbm, gain_hbm, cot_hbm, slot_hbm,
           slots_out, ctx_out, resid,
           ctx, w, res, cot, gain, slot_ref, lhs, psend, precv, own, ysum, gsend, grecv, gown,
           load_sem, w_sem, p_send, p_recv, y_send, y_recv, r_send, r_recv, g_send, g_recv, ladder):
    rows, width = resid.shape
    half = rows // 2
    chips = tensors // 2
    dp = lax.axis_index("dp")
    tensor = lax.axis_index("tensor")
    chip, core = tensor // 2, tensor % 2
    mate = chip * 2 + (1 - core)
    mine = pl.multiple_of(core * half, half)
    theirs = pl.multiple_of((1 - core) * half, half)
    count = pieces_of(width)
    cols = width // count
    chunks = half // ROWS
    bucket = slot_ref.shape[1]

    load_ctx = pltpu.make_async_copy(ctx_hbm, ctx, load_sem.at[0])
    load_ctx.start()
    loads_w = []
    for j in range(count):
        span = pl.ds(j * cols, cols)
        copy = pltpu.make_async_copy(w_hbm.at[:, span], w.at[:, span], w_sem.at[j])
        copy.start()
        loads_w.append(copy)
    load_rest = [
        pltpu.make_async_copy(res_hbm.at[pl.ds(mine, half)], res, load_sem.at[1]),
        pltpu.make_async_copy(cot_hbm.at[pl.ds(mine, half)], cot, load_sem.at[2]),
        pltpu.make_async_copy(gain_hbm, gain, load_sem.at[3]),
        pltpu.make_async_copy(slot_hbm, slot_ref, load_sem.at[4]),
    ]
    for copy in load_rest:
        copy.start()

    barrier = pltpu.get_barrier_semaphore()
    pl.semaphore_signal(barrier, inc=1, device_id={"dp": dp, "tensor": mate}, device_id_type=MESH)
    greeted = 1
    for i in range(1, chips):
        other = lax.rem(chip + i, chips) * 2 + core
        pl.semaphore_signal(barrier, inc=1, device_id={"dp": dp, "tensor": other}, device_id_type=MESH)
        greeted += 1

    lower, upper = dp >= 2, dp + 2 < replicas
    degree = 1 + lower.astype(jnp.int32) + upper.astype(jnp.int32)

    def greet(semaphore):
        pl.semaphore_signal(semaphore, inc=1, device_id={"dp": dp + 1 - 2 * lax.rem(dp, 2), "tensor": tensor},
                            device_id_type=MESH)

        @pl.when(lower)
        def _():
            pl.semaphore_signal(semaphore, inc=1, device_id={"dp": dp - 2, "tensor": tensor}, device_id_type=MESH)

        @pl.when(upper)
        def _():
            pl.semaphore_signal(semaphore, inc=1, device_id={"dp": dp + 2, "tensor": tensor}, device_id_type=MESH)

    rounds = replicas // 2 - 1 if reduce_dp else 0
    if reduce_dp:
        greet(barrier)
        greeted += degree

    load_ctx.wait()
    lhs[pl.ds(0, half)] = ctx[pl.ds(theirs, half)]
    lhs[pl.ds(half, half)] = ctx[pl.ds(mine, half)]

    def to_mate(j):
        span = pl.ds(j * cols, cols)
        return pltpu.make_async_remote_copy(
            src_ref=psend.at[:, span], dst_ref=precv.at[:, span], send_sem=p_send.at[j], recv_sem=p_recv.at[j],
            device_id={"dp": dp, "tensor": mate}, device_id_type=MESH)

    for j in range(count):
        span = pl.ds(j * cols, cols)
        loads_w[j].wait()
        product = jnp.dot(lhs[...], w[:, span], preferred_element_type=F32)
        psend[:, span] = product[:half].astype(BF16)
        own[:, span] = product[half:]
        if j == 0:
            pl.semaphore_wait(barrier, greeted)
        to_mate(j).start()
        if j == 0 and rounds:
            greet(ladder.at[0])

    def across(i, piece):
        other = lax.rem(chip + i, chips) * 2 + core
        if piece < count:
            block = ysum.at[chip, pl.ds(0, ROWS), pl.ds(piece * cols, cols)]
        else:
            block = ysum.at[chip, pl.ds((piece - count + 1) * ROWS, ROWS)]
        return pltpu.make_async_remote_copy(
            src_ref=block, dst_ref=block, send_sem=y_send.at[i - 1, piece], recv_sem=y_recv.at[i - 1, piece],
            device_id={"dp": dp, "tensor": other}, device_id_type=MESH)

    total = count + chunks - 1
    for j in range(count):
        span = pl.ds(j * cols, cols)
        to_mate(j).wait_recv()
        ysum[chip, :, span] = (own[:, span] + precv[:, span].astype(F32)).astype(BF16)
        for i in range(1, chips):
            across(i, j).start()
    for piece in range(count, total):
        for i in range(1, chips):
            across(i, piece).start()

    for copy in load_rest:
        copy.wait()
    square = (bucket, bucket)
    diagonal = lax.broadcasted_iota(jnp.int32, square, 0) == lax.broadcasted_iota(jnp.int32, square, 1)
    order = jnp.sum(jnp.where(diagonal, slot_ref[...].astype(F32), 0.0), axis=1, keepdims=True)
    place = lax.broadcasted_iota(jnp.int32, (bucket, ctx.shape[1]), 1).astype(F32)
    chosen = jnp.where(place == order, 1.0, 0.0).astype(BF16)
    picked = lax.dot_general(chosen, ctx[...], (((1,), (1,)), ((), ())),
                             preferred_element_type=F32).astype(BF16)

    def share(r):
        span = pl.ds(mine + r * ROWS, ROWS)
        return pltpu.make_async_remote_copy(
            src_ref=resid.at[span], dst_ref=resid.at[span], send_sem=r_send.at[r], recv_sem=r_recv.at[r],
            device_id={"dp": dp, "tensor": mate}, device_id_type=MESH)

    for r in range(chunks):
        for piece in (range(count) if r == 0 else (count + r - 1,)):
            for i in range(1, chips):
                across(i, piece).wait_recv()
        span = pl.ds(r * ROWS, ROWS)
        summed = ysum[0, span].astype(F32)
        for k in range(1, chips):
            summed = summed + ysum[k, span].astype(F32)
        hidden = res[span].astype(F32) + summed
        resid[pl.ds(pl.multiple_of(mine + r * ROWS, ROWS), ROWS)] = norm_backward(hidden, cot[span], gain[...])
        share(r).start()
        for turn in range(r * rounds // chunks, (r + 1) * rounds // chunks):
            pl.semaphore_wait(ladder.at[turn], degree)
            if turn + 1 < rounds:
                greet(ladder.at[turn + 1])
    for r in range(chunks):
        share(r).wait_recv()

    def to_peer(i):
        return pltpu.make_async_remote_copy(
            src_ref=gsend.at[i - 1], dst_ref=grecv.at[i - 1], send_sem=g_send.at[i - 1], recv_sem=g_recv.at[i - 1],
            device_id={"dp": lax.rem(dp + i, replicas), "tensor": tensor}, device_id_type=MESH)

    if reduce_dp:
        block = width // replicas
        for i in list(range(1, replicas)) + [0]:
            span = pl.ds(pl.multiple_of(lax.rem(dp + i, replicas) * block, block), block)
            gradient = jnp.dot(picked, resid[:, span], preferred_element_type=F32)
            if i == 0:
                gown[...] = gradient
            else:
                gsend[i - 1] = gradient.astype(BF16)
                to_peer(i).start()
    else:
        for j in range(count):
            span = pl.ds(j * cols, cols)
            slots_out[:, span] = jnp.dot(picked, resid[:, span], preferred_element_type=F32)

    back = None
    for j in range(count):
        span = pl.ds(j * cols, cols)
        term = lax.dot_general(resid[:, span], w[:, span], (((1,), (1,)), ((), ())), preferred_element_type=F32)
        back = term if back is None else back + term
    ctx_out[...] = back.astype(BF16)

    if reduce_dp:
        gradient = gown[...]
        for i in range(1, replicas):
            to_peer(i).wait_recv()
            gradient = gradient + grecv[i - 1].astype(F32)
        slots_out[...] = gradient * (1.0 / replicas)
    for j in range(count):
        to_mate(j).wait_send()
    for piece in range(total):
        for i in range(1, chips):
            across(i, piece).wait_send()
    for r in range(chunks):
        share(r).wait_send()
    if reduce_dp:
        for i in range(1, replicas):
            to_peer(i).wait_send()


def store_kernel(count, *refs):
    copies = [pltpu.make_async_copy(refs[i], refs[count + i], refs[2 * count].at[i]) for i in range(count)]
    for copy in copies:
        copy.start()
    for copy in copies:
        copy.wait()


def store(*arrays):
    count = len(arrays)
    return pl.pallas_call(
        functools.partial(store_kernel, count),
        out_shape=tuple(jax.ShapeDtypeStruct(a.shape, a.dtype) for a in arrays),
        in_specs=[ANY] * count,
        out_specs=(ANY,) * count,
        scratch_shapes=[pltpu.SemaphoreType.DMA((count,))],
        compiler_params=pltpu.CompilerParams(vmem_limit_bytes=1024 * 1024),
    )(*arrays)


def body(replicas, tensors, residual, context, w_out, gain, cotangent, slot_rows):
    micro, tokens, width = residual.shape
    depth = w_out.shape[0]
    bucket = slot_rows.shape[1]
    rows = micro * tokens
    half = rows // 2
    chips = tensors // 2
    count = pieces_of(width)
    pieces = count + half // ROWS - 1
    reduce_dp = replicas % 2 == 0 and width % (replicas * LANES) == 0
    block = width // replicas if reduce_dp else LANES
    peers = max(replicas - 1, 1) if reduce_dp else 1
    dma = pltpu.SemaphoreType.DMA
    spare = 4 * bucket * (block if reduce_dp else width) + 2 * rows * (depth + width)
    slots, ctx_grad, resid = pl.pallas_call(
        functools.partial(kernel, reduce_dp, replicas, tensors),
        out_shape=(
            pltpu.VMEM((bucket, block if reduce_dp else width), F32),
            pltpu.VMEM((rows, depth), BF16),
            pltpu.VMEM((rows, width), BF16),
        ),
        in_specs=[ANY] * 6,
        out_specs=(VMEM, VMEM, VMEM),
        scratch_shapes=[
            pltpu.VMEM((rows, depth), BF16),
            pltpu.VMEM((depth, width), BF16),
            pltpu.VMEM((half, width), BF16),
            pltpu.VMEM((half, width), BF16),
            pltpu.VMEM((1, width), F32),
            pltpu.VMEM((1, bucket), jnp.int32),
            pltpu.VMEM((rows, depth), BF16),
            pltpu.VMEM((half, width), BF16),
            pltpu.VMEM((half, width), BF16),
            pltpu.VMEM((half, width), F32),
            pltpu.VMEM((chips, half, width), BF16),
            pltpu.VMEM((peers, bucket, block), BF16),
            pltpu.VMEM((peers, bucket, block), BF16),
            pltpu.VMEM((bucket, block), F32),
            dma((5,)), dma((count,)), dma((count,)), dma((count,)),
            dma((max(chips - 1, 1), pieces)), dma((max(chips - 1, 1), pieces)),
            dma((half // ROWS,)), dma((half // ROWS,)), dma((peers,)), dma((peers,)),
            pltpu.SemaphoreType.REGULAR((max(replicas // 2 - 1, 1) if reduce_dp else 1,)),
        ],
        compiler_params=pltpu.CompilerParams(
            collective_id=0, has_side_effects=True, vmem_limit_bytes=VMEM_BYTES - spare),
    )(residual.reshape(rows, width), context.reshape(rows, depth), w_out, gain.reshape(1, width),
      cotangent.reshape(rows, width), slot_rows)
    slots, ctx_grad, resid = store(slots, ctx_grad, resid)
    if not reduce_dp:
        slots = lax.psum_scatter(slots, "dp", scatter_dimension=1, tiled=True) / replicas
    return (slots.T[None], ctx_grad.reshape(micro, tokens, depth), resid.reshape(micro, tokens, width))


def solution(mesh):
    in_specs = (
        P(None, "dp", None),
        P(None, "dp", "tensor"),
        P("tensor", None),
        P(),
        P(None, "dp", None),
        P("tensor", None),
    )
    out_specs = (P("tensor", "dp", None), P(None, "dp", "tensor"), P(None, "dp", None))
    step = functools.partial(body, mesh.shape["dp"], mesh.shape["tensor"])
    return jax.shard_map(step, mesh=mesh, in_specs=in_specs, out_specs=out_specs, check_vma=False)
```

profile of v0, /device:TPU:0, one launch (start us, length us, event | category | flops | bytes accessed | tf_op | source)
XLA Modules:
  0.0 33.2 jit_solution(11462273057442973605)
XLA Ops:
  0.6 31.4 %shard_map.85 = (f32[32,640]{1,0:T(8,128)S(1)}, bf16[128,384]{1,0:T(8,128)(2,1)S(1)}, bf16[128,5120]{1,0:T(8,128)(2,1)S(1)}) custom-call(bf16[128,5120]{1,0:T(8,128)(2,1)} %bitcast.9, bf16[128,384]{1,0:T(8,128)(2,1)} %bitcast.11, bf16[384,5120]{1,0:T(8,128)(2,1)} %w_hbm.1, f32[1,5120]{1,0:T(1,128)} %bitcast.12, bf16[128,5120]{1,0:T(8,128)(2,1)} %bitcast.10, ...), custom_call_target="tpu_custom_call" | custom-call | tf_op jit(solution)/shard_map/pallas_call | solution.py:256
  32.1 1.1 %shard_map.86 = (f32[32,640]{1,0:T(8,128)}, bf16[128,384]{1,0:T(8,128)(2,1)}, bf16[128,5120]{1,0:T(8,128)(2,1)}) custom-call(f32[32,640]{1,0:T(8,128)S(1)} %get-tuple-element.9.refs_0_, bf16[128,384]{1,0:T(8,128)(2,1)S(1)} %get-tuple-element.10.refs_1_, bf16[128,5120]{1,0:T(8,128)(2,1)S(1)} %get-tuple-element.11.refs_2_), custom_call_target="tpu_custom_call" | custom-call | tf_op jit(solution)/shard_map/pallas_call | solution.py:232
where the time goes:
time: 33.8 us; the launch traced here: 33.2 us
  Pallas kernels  32.6 us (96%)
  between operations  0.64 us (2%)
    pallas_call x1, Pallas kernels, body(): pl.pallas_call(functools.partial(kernel, reduce_dp, replicas, tensors), o...  31.4 us
    pallas_call x1, Pallas kernels, store(): pl.pallas_call(functools.partial(store_kernel, count), out_shape=tuple((j...  1.14 us

commit v1 on v0

v1 whole, which is shorter than its diff:
```python
import functools

import jax
import jax.numpy as jnp
from jax import lax
from jax.experimental import pallas as pl
from jax.experimental.pallas import tpu as pltpu
from jax.sharding import PartitionSpec as P

MESH = pl.DeviceIdType.MESH
ANY = pl.BlockSpec(memory_space=pl.ANY)
VMEM = pl.BlockSpec(memory_space=pltpu.VMEM)
F32 = jnp.float32
BF16 = jnp.bfloat16
LANES = 128
SUB = 8
VMEM_BYTES = 67043328


def pieces_of(width):
    for count in (5, 4, 2):
        if width % (count * LANES) == 0:
            return count
    return 1


def flipped(index, mask):
    bit = 1
    while bit <= mask:
        if mask & bit:
            index = index + bit * (1 - 2 * lax.rem(lax.div(index, bit), 2))
        bit *= 2
    return index


def norm_backward(hidden, cot_rows, gain):
    scale = 1.0 / hidden.shape[-1]
    center = hidden - jnp.sum(hidden, axis=-1, keepdims=True) * scale
    inverse = lax.rsqrt(jnp.sum(center * center, axis=-1, keepdims=True) * scale + 1e-05)
    upstream = cot_rows.astype(F32) * gain
    mean_up = jnp.sum(upstream, axis=-1, keepdims=True) * scale
    slope = jnp.sum(upstream * center, axis=-1, keepdims=True) * scale * inverse * inverse
    return (inverse * (upstream - mean_up - center * slope)).astype(BF16)


def kernel(reduce_dp, replicas, tensors, res_hbm, ctx_hbm, w_hbm, gain_hbm, cot_hbm, slot_hbm,
           slots_out, ctx_out, resid,
           ctx, w, res, cot, gain, slot_ref, lhs, psend, precv, own, ysend, yrecv,
           pick, pall, pat, gpick, glhs, graw, qsum, qsend, qrecv,
           load_sem, w_sem, p_send, p_recv, y_send, y_recv, a_send, a_recv, m_send, m_recv, f_send, f_recv,
           c_send, c_recv, d_send, d_recv, r_send, r_recv, q_send, q_recv, ladder):
    rows, width = resid.shape
    chips = tensors // 2
    share = rows // tensors
    nch = share // SUB
    groups = chips * nch
    far = groups - nch
    dp = lax.axis_index("dp")
    tensor = lax.axis_index("tensor")
    chip, core = tensor // 2, tensor % 2
    mate = chip * 2 + (1 - core)
    count = pieces_of(width)
    cols = width // count
    bucket = slot_ref.shape[1]
    depth = w.shape[0]
    peers = list(range(replicas - 1, 0, -1)) if reduce_dp else []
    others = list(range(1, tensors)) if reduce_dp else []

    def ahead(i):
        return lax.rem(chip + 1 + i, chips)

    def behind(i):
        return lax.rem(chip + 2 * chips - 1 - i, chips)

    load_slot = pltpu.make_async_copy(slot_hbm, slot_ref, load_sem.at[4])
    load_slot.start()
    load_ctx = pltpu.make_async_copy(ctx_hbm, ctx, load_sem.at[0])
    load_ctx.start()
    loads_w = []
    for j in range(count):
        span = pl.ds(j * cols, cols)
        copy = pltpu.make_async_copy(w_hbm.at[:, span], w.at[:, span], w_sem.at[j])
        copy.start()
        loads_w.append(copy)
    load_rest = [
        pltpu.make_async_copy(res_hbm.at[pl.ds(tensor * nch, nch)], res, load_sem.at[1]),
        pltpu.make_async_copy(cot_hbm.at[pl.ds(tensor * nch, nch)], cot, load_sem.at[2]),
        pltpu.make_async_copy(gain_hbm, gain, load_sem.at[3]),
    ]
    for copy in load_rest:
        copy.start()

    barrier = pltpu.get_barrier_semaphore()
    for i in range(1, tensors):
        pl.semaphore_signal(barrier, inc=1, device_id={"dp": dp, "tensor": lax.rem(tensor + i, tensors)},
                            device_id_type=MESH)
    greeted = tensors - 1

    lower, upper = dp >= 2, dp + 2 < replicas
    degree = 1 + lower.astype(jnp.int32) + upper.astype(jnp.int32)

    def greet(semaphore):
        pl.semaphore_signal(semaphore, inc=1, device_id={"dp": dp + 1 - 2 * lax.rem(dp, 2), "tensor": tensor},
                            device_id_type=MESH)

        @pl.when(lower)
        def _():
            pl.semaphore_signal(semaphore, inc=1, device_id={"dp": dp - 2, "tensor": tensor}, device_id_type=MESH)

        @pl.when(upper)
        def _():
            pl.semaphore_signal(semaphore, inc=1, device_id={"dp": dp + 2, "tensor": tensor}, device_id_type=MESH)

    rounds = replicas // 2 - 1 if reduce_dp else 0
    if reduce_dp:
        greet(barrier)
        greeted += degree

    load_ctx.wait()
    for i in range(chips):
        lhs[pl.ds(i * share, share)] = ctx[ahead(i) * 2 + (1 - core)]
        lhs[pl.ds((chips + i) * share, share)] = ctx[ahead(i) * 2 + core]

    load_slot.wait()
    square = (bucket, bucket)
    diagonal = lax.broadcasted_iota(jnp.int32, square, 0) == lax.broadcasted_iota(jnp.int32, square, 1)
    order = jnp.sum(jnp.where(diagonal, slot_ref[...].astype(F32), 0.0), axis=1, keepdims=True)
    place = lax.broadcasted_iota(jnp.int32, (bucket, depth), 1).astype(F32)
    chosen = jnp.where(place == order, 1.0, 0.0).astype(BF16)
    pick[...] = lax.dot_general(chosen, ctx[...].reshape(rows, depth), (((1,), (1,)), ((), ())),
                                preferred_element_type=F32).astype(BF16)

    def tell(i):
        return pltpu.make_async_remote_copy(
            src_ref=pick, dst_ref=pall.at[i - 1], send_sem=c_send.at[i - 1], recv_sem=c_recv.at[i - 1],
            device_id={"dp": dp, "tensor": lax.rem(tensor + i, tensors)}, device_id_type=MESH)

    pl.semaphore_wait(barrier, greeted)
    for i in others:
        tell(i).start()
    if rounds:
        greet(ladder.at[0])

    def to_mate(j):
        span = pl.ds(j * cols, cols)
        return pltpu.make_async_remote_copy(
            src_ref=psend.at[:, :, span], dst_ref=precv.at[:, :, span], send_sem=p_send.at[j], recv_sem=p_recv.at[j],
            device_id={"dp": dp, "tensor": mate}, device_id_type=MESH)

    for j in range(count):
        span = pl.ds(j * cols, cols)
        loads_w[j].wait()
        product = jnp.dot(lhs[...], w[:, span], preferred_element_type=F32).reshape(2 * groups, SUB, cols)
        psend[:, :, span] = product[:groups].astype(BF16)
        own[:, :, span] = product[groups:]
        to_mate(j).start()

    def across(i, piece):
        if piece < count:
            src, dst = (ref.at[i * nch, :, pl.ds(piece * cols, cols)] for ref in (ysend, yrecv))
        else:
            src, dst = (ref.at[i * nch + piece - count + 1] for ref in (ysend, yrecv))
        return pltpu.make_async_remote_copy(
            src_ref=src, dst_ref=dst, send_sem=y_send.at[i, piece], recv_sem=y_recv.at[i, piece],
            device_id={"dp": dp, "tensor": ahead(i) * 2 + core}, device_id_type=MESH)

    total = count + nch - 1
    for j in range(count):
        span = pl.ds(j * cols, cols)
        to_mate(j).wait_recv()
        ysend[:, :, span] = (own[:far, :, span] + precv[:far, :, span].astype(F32)).astype(BF16)
        for i in range(chips - 1):
            across(i, j).start()
    for piece in range(count, total):
        for i in range(chips - 1):
            across(i, piece).start()

    for copy in load_rest:
        copy.wait()
    for k in range(nch):
        own[far + k] = own[far + k] + precv[far + k].astype(F32) + res[k].astype(F32)

    def pass_pick(m):
        return pltpu.make_async_remote_copy(
            src_ref=pat.at[tensor], dst_ref=gpick.at[m - 1], send_sem=d_send.at[m - 1], recv_sem=d_recv.at[m - 1],
            device_id={"dp": flipped(dp, m), "tensor": tensor}, device_id_type=MESH)

    if reduce_dp:
        table = [None] * tensors
        for i in others:
            tell(i).wait_recv()
        for g in range(tensors):
            offset = lax.rem(tensor - g + tensors, tensors)
            block = pick[...].astype(F32)
            for i in others:
                block = jnp.where(offset == i, pall[i - 1].astype(F32), block)
            table[g] = block
        turned = jnp.concatenate(table, axis=0).T.astype(BF16)
        pat[...] = turned.reshape(tensors, share, tensors * bucket)
        gpick[replicas - 1] = pat[tensor]
        for turn in range(rounds):
            pl.semaphore_wait(ladder.at[turn], degree)
            if turn + 1 < rounds:
                greet(ladder.at[turn + 1])
        for m in peers:
            pass_pick(m).start()

    def place_of(owner, k):
        return pl.ds(pl.multiple_of((owner * nch + k) * SUB, SUB), SUB)

    def gather(i, k):
        span = place_of(tensor, k)
        return pltpu.make_async_remote_copy(
            src_ref=resid.at[span], dst_ref=resid.at[span], send_sem=a_send.at[i, k], recv_sem=a_recv.at[i, k],
            device_id={"dp": dp, "tensor": ahead(i) * 2 + core}, device_id_type=MESH)

    def beside(k):
        span = place_of(tensor, k)
        return pltpu.make_async_remote_copy(
            src_ref=resid.at[span], dst_ref=resid.at[span], send_sem=m_send.at[k], recv_sem=m_recv.at[k],
            device_id={"dp": dp, "tensor": mate}, device_id_type=MESH)

    def forward(i, k):
        span = place_of(behind(i) * 2 + core, k)
        return pltpu.make_async_remote_copy(
            src_ref=resid.at[span], dst_ref=resid.at[span], send_sem=f_send.at[i, k], recv_sem=f_recv.at[i, k],
            device_id={"dp": dp, "tensor": mate}, device_id_type=MESH)

    block = graw.shape[2]

    def columns(replica):
        return pl.ds(pl.multiple_of(replica * block, LANES), block)

    def spread(m, k):
        target = flipped(dp, m)
        return pltpu.make_async_remote_copy(
            src_ref=resid.at[place_of(tensor, k), columns(target)], dst_ref=graw.at[(m - 1) * nch + k],
            send_sem=r_send.at[m - 1, k], recv_sem=r_recv.at[m - 1, k],
            device_id={"dp": target, "tensor": tensor}, device_id_type=MESH)

    for k in range(nch):
        hidden = own[far + k]
        for i in range(chips - 1):
            for piece in (range(count) if k == 0 else (count + k - 1,)):
                across(i, piece).wait_recv()
            hidden = hidden + yrecv[i * nch + k].astype(F32)
        resid[place_of(tensor, k)] = norm_backward(hidden, cot[k], gain[...])
        for m in peers:
            spread(m, k).start()
        for i in range(chips - 1):
            gather(i, k).start()
        beside(k).start()
        if reduce_dp:
            graw[(replicas - 1) * nch + k] = resid[place_of(tensor, k), columns(dp)]

    def backward(first_owner, owners):
        span = pl.ds(pl.multiple_of(first_owner * share, share), owners * share)
        back = None
        for j in range(count):
            part = pl.ds(j * cols, cols)
            term = lax.dot_general(resid[span, part], w[:, part], (((1,), (1,)), ((), ())),
                                   preferred_element_type=F32)
            back = term if back is None else back + term
        ctx_out[span] = back.astype(BF16)

    def relay(k):
        for i in range(chips - 1):
            gather(i, k).wait_recv()
            forward(i, k).start()

    relay(0)
    for k in range(nch):
        beside(k).wait_recv()
    backward(chip * 2, 2)
    if reduce_dp:
        for m in peers:
            pass_pick(m).wait_recv()
        glhs[...] = gpick[...].reshape(replicas * share, tensors * bucket).astype(F32).T.astype(BF16)
    for k in range(1, nch - 1):
        relay(k)

    def settle(i):
        target = lax.rem(tensor + i, tensors)
        return pltpu.make_async_remote_copy(
            src_ref=qsend.at[target], dst_ref=qrecv.at[i - 1], send_sem=q_send.at[i - 1], recv_sem=q_recv.at[i - 1],
            device_id={"dp": dp, "tensor": target}, device_id_type=MESH)

    if reduce_dp:
        for m in peers:
            for k in range(nch):
                spread(m, k).wait_recv()
        tokens = graw[...].astype(F32).reshape(replicas * share, block).astype(BF16)
        gradient = jnp.dot(glhs[...], tokens, preferred_element_type=F32).reshape(tensors, bucket, block)
        qsend[...] = gradient.astype(BF16)
        for i in others:
            settle(i).start()
        qsum[...] = gradient
    relay(nch - 1)
    for i in range(chips - 1):
        for k in range(nch):
            forward(i, k).wait_recv()
        backward(behind(i) * 2, 2)

    if not reduce_dp:
        for j in range(count):
            span = pl.ds(j * cols, cols)
            slots_out[:, span] = jnp.dot(pick[...], resid[:, span], preferred_element_type=F32)

    for j in range(count):
        to_mate(j).wait_send()
    for i in range(chips - 1):
        for piece in range(total):
            across(i, piece).wait_send()
    for k in range(nch):
        for i in range(chips - 1):
            gather(i, k).wait_send()
            forward(i, k).wait_send()
        beside(k).wait_send()
    for i in others:
        tell(i).wait_send()
    for m in peers:
        pass_pick(m).wait_send()
        for k in range(nch):
            spread(m, k).wait_send()
    if reduce_dp:
        summed = qsum[tensor]
        for i in others:
            settle(i).wait_recv()
            summed = summed + qrecv[i - 1].astype(F32)
        slots_out[...] = summed * (1.0 / replicas)
        for i in others:
            settle(i).wait_send()


def store_kernel(count, *refs):
    copies = [pltpu.make_async_copy(refs[i], refs[count + i], refs[2 * count].at[i]) for i in range(count)]
    for copy in copies:
        copy.start()
    for copy in copies:
        copy.wait()


def store(*arrays):
    count = len(arrays)
    return pl.pallas_call(
        functools.partial(store_kernel, count),
        out_shape=tuple(jax.ShapeDtypeStruct(a.shape, a.dtype) for a in arrays),
        in_specs=[ANY] * count,
        out_specs=(ANY,) * count,
        scratch_shapes=[pltpu.SemaphoreType.DMA((count,))],
        compiler_params=pltpu.CompilerParams(vmem_limit_bytes=1024 * 1024),
    )(*arrays)


def body(replicas, tensors, residual, context, w_out, gain, cotangent, slot_rows):
    micro, tokens, width = residual.shape
    depth = w_out.shape[0]
    bucket = slot_rows.shape[1]
    rows = micro * tokens
    half = rows // 2
    chips = tensors // 2
    share = rows // tensors
    nch = share // SUB
    groups = chips * nch
    far = groups - nch
    count = pieces_of(width)
    pieces = count + nch - 1
    reduce_dp = (replicas > 1 and replicas & (replicas - 1) == 0 and width % (replicas * LANES) == 0
                 and rows == LANES and tensors * bucket == LANES)
    block = width // replicas if reduce_dp else LANES
    copies = replicas if reduce_dp else 1
    peers = max(copies - 1, 1)
    dma = pltpu.SemaphoreType.DMA
    spare = 4 * bucket * (block if reduce_dp else width) + 2 * rows * (depth + width)
    slots, ctx_grad, resid = pl.pallas_call(
        functools.partial(kernel, reduce_dp, replicas, tensors),
        out_shape=(
            pltpu.VMEM((bucket, block if reduce_dp else width), F32),
            pltpu.VMEM((rows, depth), BF16),
            pltpu.VMEM((rows, width), BF16),
        ),
        in_specs=[ANY] * 6,
        out_specs=(VMEM, VMEM, VMEM),
        scratch_shapes=[
            pltpu.VMEM((tensors, share, depth), BF16),
            pltpu.VMEM((depth, width), BF16),
            pltpu.VMEM((nch, SUB, width), BF16),
            pltpu.VMEM((nch, SUB, width), BF16),
            pltpu.VMEM((1, width), F32),
            pltpu.VMEM((1, bucket), jnp.int32),
            pltpu.VMEM((rows, depth), BF16),
            pltpu.VMEM((groups, SUB, width), BF16),
            pltpu.VMEM((groups, SUB, width), BF16),
            pltpu.VMEM((groups, SUB, width), F32),
            pltpu.VMEM((max(far, 1), SUB, width), BF16),
            pltpu.VMEM((max(far, 1), SUB, width), BF16),
            pltpu.VMEM((bucket, rows), BF16),
            pltpu.VMEM((tensors - 1, bucket, rows), BF16),
            pltpu.VMEM((tensors, share, tensors * bucket), BF16),
            pltpu.VMEM((copies, share, tensors * bucket), BF16),
            pltpu.VMEM((tensors * bucket, copies * share), BF16),
            pltpu.VMEM((copies * nch, SUB, block), BF16),
            pltpu.VMEM((tensors, bucket, block), F32),
            pltpu.VMEM((tensors, bucket, block), BF16),
            pltpu.VMEM((tensors - 1, bucket, block), BF16),
            dma((5,)), dma((count,)), dma((count,)), dma((count,)),
            dma((max(chips - 1, 1), pieces)), dma((max(chips - 1, 1), pieces)),
            dma((max(chips - 1, 1), nch)), dma((max(chips - 1, 1), nch)),
            dma((nch,)), dma((nch,)),
            dma((max(chips - 1, 1), nch)), dma((max(chips - 1, 1), nch)),
            dma((tensors - 1,)), dma((tensors - 1,)),
            dma((peers,)), dma((peers,)),
            dma((peers, nch)), dma((peers, nch)),
            dma((tensors - 1,)), dma((tensors - 1,)),
            pltpu.SemaphoreType.REGULAR((max(replicas // 2 - 1, 1) if reduce_dp else 1,)),
        ],
        compiler_params=pltpu.CompilerParams(
            collective_id=0, has_side_effects=True, vmem_limit_bytes=VMEM_BYTES - spare),
    )(residual.reshape(rows // SUB, SUB, width), context.reshape(tensors, share, depth), w_out, gain.reshape(1, width),
      cotangent.reshape(rows // SUB, SUB, width), slot_rows)
    slots, ctx_grad, resid = store(slots, ctx_grad, resid)
    if not reduce_dp:
        slots = lax.psum_scatter(slots, "dp", scatter_dimension=1, tiled=True) / replicas
    return (slots.T[None], ctx_grad.reshape(micro, tokens, depth), resid.reshape(micro, tokens, width))


def solution(mesh):
    in_specs = (
        P(None, "dp", None),
        P(None, "dp", "tensor"),
        P("tensor", None),
        P(),
        P(None, "dp", None),
        P("tensor", None),
    )
    out_specs = (P("tensor", "dp", None), P(None, "dp", "tensor"), P(None, "dp", None))
    step = functools.partial(body, mesh.shape["dp"], mesh.shape["tensor"])
    return jax.shard_map(step, mesh=mesh, in_specs=in_specs, out_specs=out_specs, check_vma=False)
```

time: 33.8 us -> 27.5 us (0.81); the launches traced: 33.2 us -> 27.3 us
  Pallas kernels: 32.6 us -> 26.7 us
    pallas_call x1, Pallas kernels: 31.4 us -> 25.6 us  [body(): pl.pallas_call(functools.partial(kernel, reduce_dp, replicas, tensors), o...]
where the time goes in v1:
time: 27.5 us; the launch traced here: 27.3 us
  Pallas kernels  26.7 us (97%)
  between operations  0.64 us (2%)
    pallas_call x1, Pallas kernels, body(): pl.pallas_call(functools.partial(kernel, reduce_dp, replicas, tensors), o...  25.6 us
    pallas_call x1, Pallas kernels, store(): pl.pallas_call(functools.partial(store_kernel, count), out_shape=tuple((j...  1.14 us

profile of v1, /device:TPU:0, one launch (start us, length us, event | category | flops | bytes accessed | tf_op | source)
XLA Modules:
  0.0 27.3 jit_solution(2920962513038504578)
XLA Ops:
  0.6 25.6 %shard_map.85 = (f32[32,640]{1,0:T(8,128)S(1)}, bf16[128,384]{1,0:T(8,128)(2,1)S(1)}, bf16[128,5120]{1,0:T(8,128)(2,1)S(1)}) custom-call(bf16[16,8,5120]{2,1,0:T(8,128)(2,1)} %bitcast.9, bf16[4,32,384]{2,1,0:T(8,128)(2,1)} %bitcast.11, bf16[384,5120]{1,0:T(8,128)(2,1)} %w_hbm.1, f32[1,5120]{1,0:T(1,128)} %bitcast.12, bf16[16,8,5120]{2,1,0:T(8,128)(2,1)} %bitcast.10, ...), custom_call_target="tpu_custom_call" | custom-call | tf_op jit(solution)/shard_map/pallas_call | solution.py:375
  26.2 1.1 %shard_map.86 = (f32[32,640]{1,0:T(8,128)}, bf16[128,384]{1,0:T(8,128)(2,1)}, bf16[128,5120]{1,0:T(8,128)(2,1)}) custom-call(f32[32,640]{1,0:T(8,128)S(1)} %get-tuple-element.9.refs_0_, bf16[128,384]{1,0:T(8,128)(2,1)S(1)} %get-tuple-element.10.refs_1_, bf16[128,5120]{1,0:T(8,128)(2,1)S(1)} %get-tuple-element.11.refs_2_), custom_call_target="tpu_custom_call" | custom-call | tf_op jit(solution)/shard_map/pallas_call | solution.py:345

commit v2 on v1

--- a/solution.py
+++ b/solution.py
@@ -14,6 +14,7 @@
 BF16 = jnp.bfloat16
 LANES = 128
 SUB = 8
+LAG = 3
 VMEM_BYTES = 67043328
 
 
@@ -121,60 +122,76 @@
         lhs[pl.ds(i * share, share)] = ctx[ahead(i) * 2 + (1 - core)]
         lhs[pl.ds((chips + i) * share, share)] = ctx[ahead(i) * 2 + core]
 
-    load_slot.wait()
-    square = (bucket, bucket)
-    diagonal = lax.broadcasted_iota(jnp.int32, square, 0) == lax.broadcasted_iota(jnp.int32, square, 1)
-    order = jnp.sum(jnp.where(diagonal, slot_ref[...].astype(F32), 0.0), axis=1, keepdims=True)
-    place = lax.broadcasted_iota(jnp.int32, (bucket, depth), 1).astype(F32)
-    chosen = jnp.where(place == order, 1.0, 0.0).astype(BF16)
-    pick[...] = lax.dot_general(chosen, ctx[...].reshape(rows, depth), (((1,), (1,)), ((), ())),
-                                preferred_element_type=F32).astype(BF16)
-
-    def tell(i):
-        return pltpu.make_async_remote_copy(
-            src_ref=pick, dst_ref=pall.at[i - 1], send_sem=c_send.at[i - 1], recv_sem=c_recv.at[i - 1],
-            device_id={"dp": dp, "tensor": lax.rem(tensor + i, tensors)}, device_id_type=MESH)
-
-    pl.semaphore_wait(barrier, greeted)
-    for i in others:
-        tell(i).start()
-    if rounds:
-        greet(ladder.at[0])
-
     def to_mate(j):
         span = pl.ds(j * cols, cols)
         return pltpu.make_async_remote_copy(
-            src_ref=psend.at[:, :, span], dst_ref=precv.at[:, :, span], send_sem=p_send.at[j], recv_sem=p_recv.at[j],
+            src_ref=psend.at[:, :, span], dst_ref=precv.at[:, :, span], send_sem=p_send, recv_sem=p_recv.at[j],
             device_id={"dp": dp, "tensor": mate}, device_id_type=MESH)
 
+    def tell(i):
+        return pltpu.make_async_remote_copy(
+            src_ref=pick, dst_ref=pall.at[i - 1], send_sem=c_send, recv_sem=c_recv,
+            device_id={"dp": dp, "tensor": lax.rem(tensor + i, tensors)}, device_id_type=MESH)
+
+    def across(i, piece):
+        if piece < count:
+            src, dst = (ref.at[i * nch, :, pl.ds(piece * cols, cols)] for ref in (ysend, yrecv))
+        else:
+            src, dst = (ref.at[i * nch + piece - count + 1] for ref in (ysend, yrecv))
+        return pltpu.make_async_remote_copy(
+            src_ref=src, dst_ref=dst, send_sem=y_send, recv_sem=y_recv.at[i, max(piece - count + 1, 0)],
+            device_id={"dp": dp, "tensor": ahead(i) * 2 + core}, device_id_type=MESH)
+
+    def merge(j):
+        span = pl.ds(j * cols, cols)
+        to_mate(j).wait_recv()
+        ysend[:, :, span] = (own[:far, :, span] + precv[:far, :, span].astype(F32)).astype(BF16)
+        for i in range(chips - 1):
+            across(i, j).start()
+
+    def whole(ref, send, recv):
+        return pltpu.make_async_remote_copy(
+            src_ref=ref, dst_ref=ref, send_sem=send, recv_sem=recv,
+            device_id={"dp": dp, "tensor": mate}, device_id_type=MESH)
+
+    total = count + nch - 1
     for j in range(count):
         span = pl.ds(j * cols, cols)
         loads_w[j].wait()
         product = jnp.dot(lhs[...], w[:, span], preferred_element_type=F32).reshape(2 * groups, SUB, cols)
         psend[:, :, span] = product[:groups].astype(BF16)
         own[:, :, span] = product[groups:]
+        if j == 0:
+            pl.semaphore_wait(barrier, greeted)
         to_mate(j).start()
-
-    def across(i, piece):
-        if piece < count:
-            src, dst = (ref.at[i * nch, :, pl.ds(piece * cols, cols)] for ref in (ysend, yrecv))
-        else:
-            src, dst = (ref.at[i * nch + piece - count + 1] for ref in (ysend, yrecv))
-        return pltpu.make_async_remote_copy(
-            src_ref=src, dst_ref=dst, send_sem=y_send.at[i, piece], recv_sem=y_recv.at[i, piece],
-            device_id={"dp": dp, "tensor": ahead(i) * 2 + core}, device_id_type=MESH)
-
-    total = count + nch - 1
-    for j in range(count):
-        span = pl.ds(j * cols, cols)
-        to_mate(j).wait_recv()
-        ysend[:, :, span] = (own[:far, :, span] + precv[:far, :, span].astype(F32)).astype(BF16)
-        for i in range(chips - 1):
-            across(i, j).start()
+        if j == 0 and rounds:
+            greet(ladder.at[0])
+        if j == min(1, count - 1):
+            load_slot.wait()
+            square = (bucket, bucket)
+            diagonal = lax.broadcasted_iota(jnp.int32, square, 0) == lax.broadcasted_iota(jnp.int32, square, 1)
+            order = jnp.sum(jnp.where(diagonal, slot_ref[...].astype(F32), 0.0), axis=1, keepdims=True)
+            place = lax.broadcasted_iota(jnp.int32, (bucket, depth), 1).astype(F32)
+            chosen = jnp.where(place == order, 1.0, 0.0).astype(BF16)
+            pick[...] = lax.dot_general(chosen, ctx[...].reshape(rows, depth), (((1,), (1,)), ((), ())),
+                                        preferred_element_type=F32).astype(BF16)
+            for i in others:
+                tell(i).start()
+        if j >= LAG:
+            merge(j - LAG)
+    for j in range(max(count - LAG, 0), count):
+        merge(j)
     for piece in range(count, total):
         for i in range(chips - 1):
             across(i, piece).start()
 
+    def climb(turn):
+        pl.semaphore_wait(ladder.at[turn], degree)
+        if turn + 1 < rounds:
+            greet(ladder.at[turn + 1])
+
+    if rounds:
+        climb(0)
     for copy in load_rest:
         copy.wait()
     for k in range(nch):
@@ -182,13 +199,12 @@
 
     def pass_pick(m):
         return pltpu.make_async_remote_copy(
-            src_ref=pat.at[tensor], dst_ref=gpick.at[m - 1], send_sem=d_send.at[m - 1], recv_sem=d_recv.at[m - 1],
+            src_ref=pat.at[tensor], dst_ref=gpick.at[m - 1], send_sem=d_send, recv_sem=d_recv,
             device_id={"dp": flipped(dp, m), "tensor": tensor}, device_id_type=MESH)
 
     if reduce_dp:
         table = [None] * tensors
-        for i in others:
-            tell(i).wait_recv()
+        whole(pall, c_send, c_recv).wait_recv()
         for g in range(tensors):
             offset = lax.rem(tensor - g + tensors, tensors)
             block = pick[...].astype(F32)
@@ -198,10 +214,8 @@
         turned = jnp.concatenate(table, axis=0).T.astype(BF16)
         pat[...] = turned.reshape(tensors, share, tensors * bucket)
         gpick[replicas - 1] = pat[tensor]
-        for turn in range(rounds):
-            pl.semaphore_wait(ladder.at[turn], degree)
-            if turn + 1 < rounds:
-                greet(ladder.at[turn + 1])
+        for turn in range(1, rounds):
+            climb(turn)
         for m in peers:
             pass_pick(m).start()
 
@@ -211,19 +225,19 @@
     def gather(i, k):
         span = place_of(tensor, k)
         return pltpu.make_async_remote_copy(
-            src_ref=resid.at[span], dst_ref=resid.at[span], send_sem=a_send.at[i, k], recv_sem=a_recv.at[i, k],
+            src_ref=resid.at[span], dst_ref=resid.at[span], send_sem=a_send, recv_sem=a_recv.at[i, k],
             device_id={"dp": dp, "tensor": ahead(i) * 2 + core}, device_id_type=MESH)
 
     def beside(k):
         span = place_of(tensor, k)
         return pltpu.make_async_remote_copy(
-            src_ref=resid.at[span], dst_ref=resid.at[span], send_sem=m_send.at[k], recv_sem=m_recv.at[k],
+            src_ref=resid.at[span], dst_ref=resid.at[span], send_sem=m_send, recv_sem=m_recv,
             device_id={"dp": dp, "tensor": mate}, device_id_type=MESH)
 
     def forward(i, k):
         span = place_of(behind(i) * 2 + core, k)
         return pltpu.make_async_remote_copy(
-            src_ref=resid.at[span], dst_ref=resid.at[span], send_sem=f_send.at[i, k], recv_sem=f_recv.at[i, k],
+            src_ref=resid.at[span], dst_ref=resid.at[span], send_sem=f_send, recv_sem=f_recv,
             device_id={"dp": dp, "tensor": mate}, device_id_type=MESH)
 
     block = graw.shape[2]
@@ -235,14 +249,13 @@
         target = flipped(dp, m)
         return pltpu.make_async_remote_copy(
             src_ref=resid.at[place_of(tensor, k), columns(target)], dst_ref=graw.at[(m - 1) * nch + k],
-            send_sem=r_send.at[m - 1, k], recv_sem=r_recv.at[m - 1, k],
+            send_sem=r_send, recv_sem=r_recv,
             device_id={"dp": target, "tensor": tensor}, device_id_type=MESH)
 
     for k in range(nch):
         hidden = own[far + k]
         for i in range(chips - 1):
-            for piece in (range(count) if k == 0 else (count + k - 1,)):
-                across(i, piece).wait_recv()
+            whole(yrecv.at[i * nch + k], y_send, y_recv.at[i, k]).wait_recv()
             hidden = hidden + yrecv[i * nch + k].astype(F32)
         resid[place_of(tensor, k)] = norm_backward(hidden, cot[k], gain[...])
         for m in peers:
@@ -269,12 +282,10 @@
             forward(i, k).start()
 
     relay(0)
-    for k in range(nch):
-        beside(k).wait_recv()
+    whole(res, m_send, m_recv).wait_recv()
     backward(chip * 2, 2)
     if reduce_dp:
-        for m in peers:
-            pass_pick(m).wait_recv()
+        whole(gpick.at[pl.ds(0, replicas - 1)], d_send, d_recv).wait_recv()
         glhs[...] = gpick[...].reshape(replicas * share, tensors * bucket).astype(F32).T.astype(BF16)
     for k in range(1, nch - 1):
         relay(k)
@@ -282,13 +293,11 @@
     def settle(i):
         target = lax.rem(tensor + i, tensors)
         return pltpu.make_async_remote_copy(
-            src_ref=qsend.at[target], dst_ref=qrecv.at[i - 1], send_sem=q_send.at[i - 1], recv_sem=q_recv.at[i - 1],
+            src_ref=qsend.at[target], dst_ref=qrecv.at[i - 1], send_sem=q_send, recv_sem=q_recv,
             device_id={"dp": dp, "tensor": target}, device_id_type=MESH)
 
     if reduce_dp:
-        for m in peers:
-            for k in range(nch):
-                spread(m, k).wait_recv()
+        whole(graw.at[pl.ds(0, (replicas - 1) * nch)], r_send, r_recv).wait_recv()
         tokens = graw[...].astype(F32).reshape(replicas * share, block).astype(BF16)
         gradient = jnp.dot(glhs[...], tokens, preferred_element_type=F32).reshape(tensors, bucket, block)
         qsend[...] = gradient.astype(BF16)
@@ -296,9 +305,9 @@
             settle(i).start()
         qsum[...] = gradient
     relay(nch - 1)
+    if far:
+        whole(ysend, f_send, f_recv).wait_recv()
     for i in range(chips - 1):
-        for k in range(nch):
-            forward(i, k).wait_recv()
         backward(behind(i) * 2, 2)
 
     if not reduce_dp:
@@ -306,30 +315,21 @@
             span = pl.ds(j * cols, cols)
             slots_out[:, span] = jnp.dot(pick[...], resid[:, span], preferred_element_type=F32)
 
-    for j in range(count):
-        to_mate(j).wait_send()
-    for i in range(chips - 1):
-        for piece in range(total):
-            across(i, piece).wait_send()
-    for k in range(nch):
-        for i in range(chips - 1):
-            gather(i, k).wait_send()
-            forward(i, k).wait_send()
-        beside(k).wait_send()
-    for i in others:
-        tell(i).wait_send()
-    for m in peers:
-        pass_pick(m).wait_send()
-        for k in range(nch):
-            spread(m, k).wait_send()
+    whole(psend, p_send, p_recv.at[0]).wait_send()
+    if far:
+        for semaphore in (y_send, a_send, f_send):
+            whole(ysend, semaphore, f_recv).wait_send()
+    whole(res, m_send, m_recv).wait_send()
     if reduce_dp:
+        whole(pall, c_send, c_recv).wait_send()
+        whole(gpick.at[pl.ds(0, replicas - 1)], d_send, d_recv).wait_send()
+        whole(graw.at[pl.ds(0, (replicas - 1) * nch)], r_send, r_recv).wait_send()
+        whole(qrecv, q_send, q_recv).wait_recv()
         summed = qsum[tensor]
         for i in others:
-            settle(i).wait_recv()
             summed = summed + qrecv[i - 1].astype(F32)
         slots_out[...] = summed * (1.0 / replicas)
-        for i in others:
-            settle(i).wait_send()
+        whole(qrecv, q_send, q_recv).wait_send()
 
 
 def store_kernel(count, *refs):
@@ -364,12 +364,10 @@
     groups = chips * nch
     far = groups - nch
     count = pieces_of(width)
-    pieces = count + nch - 1
     reduce_dp = (replicas > 1 and replicas & (replicas - 1) == 0 and width % (replicas * LANES) == 0
                  and rows == LANES and tensors * bucket == LANES)
     block = width // replicas if reduce_dp else LANES
     copies = replicas if reduce_dp else 1
-    peers = max(copies - 1, 1)
     dma = pltpu.SemaphoreType.DMA
     spare = 4 * bucket * (block if reduce_dp else width) + 2 * rows * (depth + width)
     slots, ctx_grad, resid = pl.pallas_call(
@@ -403,15 +401,10 @@
             pltpu.VMEM((tensors, bucket, block), F32),
             pltpu.VMEM((tensors, bucket, block), BF16),
             pltpu.VMEM((tensors - 1, bucket, block), BF16),
-            dma((5,)), dma((count,)), dma((count,)), dma((count,)),
-            dma((max(chips - 1, 1), pieces)), dma((max(chips - 1, 1), pieces)),
-            dma((max(chips - 1, 1), nch)), dma((max(chips - 1, 1), nch)),
-            dma((nch,)), dma((nch,)),
-            dma((max(chips - 1, 1), nch)), dma((max(chips - 1, 1), nch)),
-            dma((tensors - 1,)), dma((tensors - 1,)),
-            dma((peers,)), dma((peers,)),
-            dma((peers, nch)), dma((peers, nch)),
-            dma((tensors - 1,)), dma((tensors - 1,)),
+            dma((5,)), dma((count,)), dma, dma((count,)),
+            dma, dma((max(chips - 1, 1), nch)),
+            dma, dma((max(chips - 1, 1), nch)),
+            dma, dma, dma, dma, dma, dma, dma, dma, dma, dma, dma, dma,
             pltpu.SemaphoreType.REGULAR((max(replicas // 2 - 1, 1) if reduce_dp else 1,)),
         ],
         compiler_params=pltpu.CompilerParams(

time: 27.5 us -> 26.5 us (0.964)
  Pallas kernels: 26.7 us -> 25.7 us
    pallas_call x1, Pallas kernels: 25.6 us -> 24.6 us  [body(): pl.pallas_call(functools.partial(kernel, reduce_dp, replicas, tensors), o...]
where the time goes in v2:
time: 26.5 us; the launch traced here: 26.4 us
  Pallas kernels  25.7 us (97%)
  between operations  0.64 us (2%)
    pallas_call x1, Pallas kernels, body(): pl.pallas_call(functools.partial(kernel, reduce_dp, replicas, tensors), o...  24.6 us
    pallas_call x1, Pallas kernels, store(): pl.pallas_call(functools.partial(store_kernel, count), out_shape=tuple((j...  1.14 us

profile of v2, /device:TPU:0, one launch (start us, length us, event | category | flops | bytes accessed | tf_op | source)
XLA Modules:
  0.0 26.4 jit_solution(12085408834375433467)
XLA Ops:
  0.6 24.6 %shard_map.85 = (f32[32,640]{1,0:T(8,128)S(1)}, bf16[128,384]{1,0:T(8,128)(2,1)S(1)}, bf16[128,5120]{1,0:T(8,128)(2,1)S(1)}) custom-call(bf16[16,8,5120]{2,1,0:T(8,128)(2,1)} %bitcast.9, bf16[4,32,384]{2,1,0:T(8,128)(2,1)} %bitcast.11, bf16[384,5120]{1,0:T(8,128)(2,1)} %w_hbm.1, f32[1,5120]{1,0:T(1,128)} %bitcast.12, bf16[16,8,5120]{2,1,0:T(8,128)(2,1)} %bitcast.10, ...), custom_call_target="tpu_custom_call" | custom-call | tf_op jit(solution)/shard_map/pallas_call | solution.py:373
  25.2 1.1 %shard_map.86 = (f32[32,640]{1,0:T(8,128)}, bf16[128,384]{1,0:T(8,128)(2,1)}, bf16[128,5120]{1,0:T(8,128)(2,1)}) custom-call(f32[32,640]{1,0:T(8,128)S(1)} %get-tuple-element.9.refs_0_, bf16[128,384]{1,0:T(8,128)(2,1)S(1)} %get-tuple-element.10.refs_1_, bf16[128,5120]{1,0:T(8,128)(2,1)S(1)} %get-tuple-element.11.refs_2_), custom_call_target="tpu_custom_call" | custom-call | tf_op jit(solution)/shard_map/pallas_call | solution.py:345

commit v3 on v2

--- a/solution.py
+++ b/solution.py
@@ -149,6 +149,11 @@
         for i in range(chips - 1):
             across(i, j).start()
 
+    def climb(turn):
+        pl.semaphore_wait(ladder.at[turn], degree)
+        if turn + 1 < rounds:
+            greet(ladder.at[turn + 1])
+
     def whole(ref, send, recv):
         return pltpu.make_async_remote_copy(
             src_ref=ref, dst_ref=ref, send_sem=send, recv_sem=recv,
@@ -162,11 +167,6 @@
         psend[:, :, span] = product[:groups].astype(BF16)
         own[:, :, span] = product[groups:]
         if j == 0:
-            pl.semaphore_wait(barrier, greeted)
-        to_mate(j).start()
-        if j == 0 and rounds:
-            greet(ladder.at[0])
-        if j == min(1, count - 1):
             load_slot.wait()
             square = (bucket, bucket)
             diagonal = lax.broadcasted_iota(jnp.int32, square, 0) == lax.broadcasted_iota(jnp.int32, square, 1)
@@ -175,23 +175,27 @@
             chosen = jnp.where(place == order, 1.0, 0.0).astype(BF16)
             pick[...] = lax.dot_general(chosen, ctx[...].reshape(rows, depth), (((1,), (1,)), ((), ())),
                                         preferred_element_type=F32).astype(BF16)
+            pl.semaphore_wait(barrier, greeted)
+        to_mate(j).start()
+        if j == 0:
+            if rounds:
+                greet(ladder.at[0])
             for i in others:
                 tell(i).start()
+        if j == LAG and rounds:
+            climb(0)
         if j >= LAG:
             merge(j - LAG)
+    if rounds and count <= LAG:
+        climb(0)
     for j in range(max(count - LAG, 0), count):
+        if j == count - 1 and rounds > 1:
+            climb(1)
         merge(j)
     for piece in range(count, total):
         for i in range(chips - 1):
             across(i, piece).start()
 
-    def climb(turn):
-        pl.semaphore_wait(ladder.at[turn], degree)
-        if turn + 1 < rounds:
-            greet(ladder.at[turn + 1])
-
-    if rounds:
-        climb(0)
     for copy in load_rest:
         copy.wait()
     for k in range(nch):
@@ -214,7 +218,7 @@
         turned = jnp.concatenate(table, axis=0).T.astype(BF16)
         pat[...] = turned.reshape(tensors, share, tensors * bucket)
         gpick[replicas - 1] = pat[tensor]
-        for turn in range(1, rounds):
+        for turn in range(2, rounds):
             climb(turn)
         for m in peers:
             pass_pick(m).start()
@@ -222,10 +226,17 @@
     def place_of(owner, k):
         return pl.ds(pl.multiple_of((owner * nch + k) * SUB, SUB), SUB)
 
-    def gather(i, k):
-        span = place_of(tensor, k)
-        return pltpu.make_async_remote_copy(
-            src_ref=resid.at[span], dst_ref=resid.at[span], send_sem=a_send, recv_sem=a_recv.at[i, k],
+    last = nch - 1
+
+    def part_of(owner, piece):
+        if piece < last:
+            return resid.at[place_of(owner, piece)]
+        return resid.at[place_of(owner, last), pl.ds((piece - last) * cols, cols)]
+
+    def gather(i, piece):
+        part = part_of(tensor, piece)
+        return pltpu.make_async_remote_copy(
+            src_ref=part, dst_ref=part, send_sem=a_send, recv_sem=a_recv.at[i, piece],
             device_id={"dp": dp, "tensor": ahead(i) * 2 + core}, device_id_type=MESH)
 
     def beside(k):
@@ -234,10 +245,10 @@
             src_ref=resid.at[span], dst_ref=resid.at[span], send_sem=m_send, recv_sem=m_recv,
             device_id={"dp": dp, "tensor": mate}, device_id_type=MESH)
 
-    def forward(i, k):
-        span = place_of(behind(i) * 2 + core, k)
-        return pltpu.make_async_remote_copy(
-            src_ref=resid.at[span], dst_ref=resid.at[span], send_sem=f_send, recv_sem=f_recv,
+    def forward(i, piece):
+        part = part_of(behind(i) * 2 + core, piece)
+        return pltpu.make_async_remote_copy(
+            src_ref=part, dst_ref=part, send_sem=f_send, recv_sem=f_recv.at[i, max(piece - last + 1, 0)],
             device_id={"dp": dp, "tensor": mate}, device_id_type=MESH)
 
     block = graw.shape[2]
@@ -261,33 +272,36 @@
         for m in peers:
             spread(m, k).start()
         for i in range(chips - 1):
-            gather(i, k).start()
+            for piece in (range(last, last + count) if k == last else (k,)):
+                gather(i, piece).start()
         beside(k).start()
         if reduce_dp:
             graw[(replicas - 1) * nch + k] = resid[place_of(tensor, k), columns(dp)]
 
-    def backward(first_owner, owners):
-        span = pl.ds(pl.multiple_of(first_owner * share, share), owners * share)
-        back = None
-        for j in range(count):
-            part = pl.ds(j * cols, cols)
-            term = lax.dot_general(resid[span, part], w[:, part], (((1,), (1,)), ((), ())),
-                                   preferred_element_type=F32)
-            back = term if back is None else back + term
-        ctx_out[span] = back.astype(BF16)
-
-    def relay(k):
-        for i in range(chips - 1):
-            gather(i, k).wait_recv()
-            forward(i, k).start()
-
-    relay(0)
+    def rows_of(owner):
+        return pl.ds(pl.multiple_of(owner * share, share), 2 * share)
+
+    def backward(span, j):
+        part = pl.ds(j * cols, cols)
+        return lax.dot_general(resid[span, part], w[:, part], (((1,), (1,)), ((), ())), preferred_element_type=F32)
+
+    def relay(piece):
+        for i in range(chips - 1):
+            gather(i, piece).wait_recv()
+            forward(i, piece).start()
+
+    if last:
+        relay(0)
     whole(res, m_send, m_recv).wait_recv()
-    backward(chip * 2, 2)
+    span = rows_of(chip * 2)
+    back = backward(span, 0)
+    for j in range(1, count):
+        back = back + backward(span, j)
+    ctx_out[span] = back.astype(BF16)
     if reduce_dp:
         whole(gpick.at[pl.ds(0, replicas - 1)], d_send, d_recv).wait_recv()
         glhs[...] = gpick[...].reshape(replicas * share, tensors * bucket).astype(F32).T.astype(BF16)
-    for k in range(1, nch - 1):
+    for k in range(1, last):
         relay(k)
 
     def settle(i):
@@ -304,11 +318,20 @@
         for i in others:
             settle(i).start()
         qsum[...] = gradient
-    relay(nch - 1)
-    if far:
-        whole(ysend, f_send, f_recv).wait_recv()
+    for j in range(count - 1):
+        relay(last + j)
+    backs = [None] * (chips - 1)
+    for j in range(count):
+        for i in range(chips - 1):
+            if j == 0 and last:
+                whole(ysend.at[pl.ds(0, last)], f_send, f_recv.at[i, 0]).wait_recv()
+            forward(i, last + j).wait_recv()
+            term = backward(rows_of(behind(i) * 2), j)
+            backs[i] = term if j == 0 else backs[i] + term
+        if j == 0:
+            relay(last + count - 1)
     for i in range(chips - 1):
-        backward(behind(i) * 2, 2)
+        ctx_out[rows_of(behind(i) * 2)] = backs[i].astype(BF16)
 
     if not reduce_dp:
         for j in range(count):
@@ -318,7 +341,7 @@
     whole(psend, p_send, p_recv.at[0]).wait_send()
     if far:
         for semaphore in (y_send, a_send, f_send):
-            whole(ysend, semaphore, f_recv).wait_send()
+            whole(ysend, semaphore, m_recv).wait_send()
     whole(res, m_send, m_recv).wait_send()
     if reduce_dp:
         whole(pall, c_send, c_recv).wait_send()
@@ -403,8 +426,9 @@
             pltpu.VMEM((tensors - 1, bucket, block), BF16),
             dma((5,)), dma((count,)), dma, dma((count,)),
             dma, dma((max(chips - 1, 1), nch)),
-            dma, dma((max(chips - 1, 1), nch)),
-            dma, dma, dma, dma, dma, dma, dma, dma, dma, dma, dma, dma,
+            dma, dma((max(chips - 1, 1), nch - 1 + count)),
+            dma, dma, dma, dma((max(chips - 1, 1), 1 + count)),
+            dma, dma, dma, dma, dma, dma, dma, dma,
             pltpu.SemaphoreType.REGULAR((max(replicas // 2 - 1, 1) if reduce_dp else 1,)),
         ],
         compiler_params=pltpu.CompilerParams(

time: 26.5 us -> 26.2 us (0.989)
  Pallas kernels: 25.7 us -> 25.2 us
    pallas_call x1, Pallas kernels: 24.6 us -> 24.1 us  [body(): pl.pallas_call(functools.partial(kernel, reduce_dp, replicas, tensors), o...]
where the time goes in v3:
time: 26.2 us; the launch traced here: 25.9 us
  Pallas kernels  25.2 us (96%)
  between operations  0.64 us (2%)
    pallas_call x1, Pallas kernels, body(): pl.pallas_call(functools.partial(kernel, reduce_dp, replicas, tensors), o...  24.1 us
    pallas_call x1, Pallas kernels, store(): pl.pallas_call(functools.partial(store_kernel, count), out_shape=tuple((j...  1.14 us

profile of v3, /device:TPU:0, one launch (start us, length us, event | category | flops | bytes accessed | tf_op | source)
XLA Modules:
  0.0 25.9 jit_solution(2433007478493926276)
XLA Ops:
  0.6 24.1 %shard_map.85 = (f32[32,640]{1,0:T(8,128)S(1)}, bf16[128,384]{1,0:T(8,128)(2,1)S(1)}, bf16[128,5120]{1,0:T(8,128)(2,1)S(1)}) custom-call(bf16[16,8,5120]{2,1,0:T(8,128)(2,1)} %bitcast.9, bf16[4,32,384]{2,1,0:T(8,128)(2,1)} %bitcast.11, bf16[384,5120]{1,0:T(8,128)(2,1)} %w_hbm.1, f32[1,5120]{1,0:T(1,128)} %bitcast.12, bf16[16,8,5120]{2,1,0:T(8,128)(2,1)} %bitcast.10, ...), custom_call_target="tpu_custom_call" | custom-call | tf_op jit(solution)/shard_map/pallas_call | solution.py:396
  24.7 1.1 %shard_map.86 = (f32[32,640]{1,0:T(8,128)}, bf16[128,384]{1,0:T(8,128)(2,1)}, bf16[128,5120]{1,0:T(8,128)(2,1)}) custom-call(f32[32,640]{1,0:T(8,128)S(1)} %get-tuple-element.9.refs_0_, bf16[128,384]{1,0:T(8,128)(2,1)S(1)} %get-tuple-element.10.refs_1_, bf16[128,5120]{1,0:T(8,128)(2,1)S(1)} %get-tuple-element.11.refs_2_), custom_call_target="tpu_custom_call" | custom-call | tf_op jit(solution)/shard_map/pallas_call | solution.py:368

commit v4 on v3

--- a/solution.py
+++ b/solution.py
@@ -46,7 +46,7 @@
 
 def kernel(reduce_dp, replicas, tensors, res_hbm, ctx_hbm, w_hbm, gain_hbm, cot_hbm, slot_hbm,
            slots_out, ctx_out, resid,
-           ctx, w, res, cot, gain, slot_ref, lhs, psend, precv, own, ysend, yrecv,
+           ctx, w, wt, res, cot, gain, slot_ref, lhs, psend, precv, own, ysend, yrecv,
            pick, pall, pat, gpick, glhs, graw, qsum, qsend, qrecv,
            load_sem, w_sem, p_send, p_recv, y_send, y_recv, a_send, a_recv, m_send, m_recv, f_send, f_recv,
            c_send, c_recv, d_send, d_recv, r_send, r_recv, q_send, q_recv, ladder):
@@ -97,25 +97,31 @@
                             device_id_type=MESH)
     greeted = tensors - 1
 
-    lower, upper = dp >= 2, dp + 2 < replicas
-    degree = 1 + lower.astype(jnp.int32) + upper.astype(jnp.int32)
-
-    def greet(semaphore):
-        pl.semaphore_signal(semaphore, inc=1, device_id={"dp": dp + 1 - 2 * lax.rem(dp, 2), "tensor": tensor},
-                            device_id_type=MESH)
-
-        @pl.when(lower)
+    def greet(semaphore, reach):
+        if reach == 1:
+            pl.semaphore_signal(semaphore, inc=1, device_id={"dp": dp + 1 - 2 * lax.rem(dp, 2), "tensor": tensor},
+                                device_id_type=MESH)
+
+        @pl.when(dp >= 2 * reach)
         def _():
-            pl.semaphore_signal(semaphore, inc=1, device_id={"dp": dp - 2, "tensor": tensor}, device_id_type=MESH)
-
-        @pl.when(upper)
+            pl.semaphore_signal(semaphore, inc=1, device_id={"dp": dp - 2 * reach, "tensor": tensor},
+                                device_id_type=MESH)
+
+        @pl.when(dp + 2 * reach < replicas)
         def _():
-            pl.semaphore_signal(semaphore, inc=1, device_id={"dp": dp + 2, "tensor": tensor}, device_id_type=MESH)
-
-    rounds = replicas // 2 - 1 if reduce_dp else 0
+            pl.semaphore_signal(semaphore, inc=1, device_id={"dp": dp + 2 * reach, "tensor": tensor},
+                                device_id_type=MESH)
+
+    def degree(reach):
+        near = (dp >= 2 * reach).astype(jnp.int32) + (dp + 2 * reach < replicas).astype(jnp.int32)
+        return near + 1 if reach == 1 else near
+
+    reaches = []
+    while reduce_dp and 2 ** len(reaches) < replicas // 2:
+        reaches.append(2 ** len(reaches))
     if reduce_dp:
-        greet(barrier)
-        greeted += degree
+        greet(barrier, 1)
+        greeted += degree(1)
 
     load_ctx.wait()
     for i in range(chips):
@@ -150,9 +156,10 @@
             across(i, j).start()
 
     def climb(turn):
-        pl.semaphore_wait(ladder.at[turn], degree)
-        if turn + 1 < rounds:
-            greet(ladder.at[turn + 1])
+        if turn < len(reaches):
+            pl.semaphore_wait(ladder.at[turn], degree(reaches[turn]))
+        if turn + 1 < len(reaches):
+            greet(ladder.at[turn + 1], reaches[turn + 1])
 
     def whole(ref, send, recv):
         return pltpu.make_async_remote_copy(
@@ -178,19 +185,15 @@
             pl.semaphore_wait(barrier, greeted)
         to_mate(j).start()
         if j == 0:
-            if rounds:
-                greet(ladder.at[0])
+            if reaches:
+                greet(ladder.at[0], 1)
             for i in others:
                 tell(i).start()
-        if j == LAG and rounds:
-            climb(0)
         if j >= LAG:
             merge(j - LAG)
-    if rounds and count <= LAG:
-        climb(0)
     for j in range(max(count - LAG, 0), count):
-        if j == count - 1 and rounds > 1:
-            climb(1)
+        if j == count - 1:
+            climb(0)
         merge(j)
     for piece in range(count, total):
         for i in range(chips - 1):
@@ -218,7 +221,7 @@
         turned = jnp.concatenate(table, axis=0).T.astype(BF16)
         pat[...] = turned.reshape(tensors, share, tensors * bucket)
         gpick[replicas - 1] = pat[tensor]
-        for turn in range(2, rounds):
+        for turn in range(1, len(reaches)):
             climb(turn)
         for m in peers:
             pass_pick(m).start()
@@ -275,6 +278,9 @@
             for piece in (range(last, last + count) if k == last else (k,)):
                 gather(i, piece).start()
         beside(k).start()
+        for j in range(k * count // nch, (k + 1) * count // nch):
+            span = pl.ds(j * cols, cols)
+            wt[span] = w[:, span].T
         if reduce_dp:
             graw[(replicas - 1) * nch + k] = resid[place_of(tensor, k), columns(dp)]
 
@@ -283,7 +289,7 @@
 
     def backward(span, j):
         part = pl.ds(j * cols, cols)
-        return lax.dot_general(resid[span, part], w[:, part], (((1,), (1,)), ((), ())), preferred_element_type=F32)
+        return jnp.dot(resid[span, part], wt[part], preferred_element_type=F32)
 
     def relay(piece):
         for i in range(chips - 1):
@@ -318,7 +324,7 @@
         for i in others:
             settle(i).start()
         qsum[...] = gradient
-    for j in range(count - 1):
+    for j in range(count):
         relay(last + j)
     backs = [None] * (chips - 1)
     for j in range(count):
@@ -328,8 +334,6 @@
             forward(i, last + j).wait_recv()
             term = backward(rows_of(behind(i) * 2), j)
             backs[i] = term if j == 0 else backs[i] + term
-        if j == 0:
-            relay(last + count - 1)
     for i in range(chips - 1):
         ctx_out[rows_of(behind(i) * 2)] = backs[i].astype(BF16)
 
@@ -405,6 +409,7 @@
         scratch_shapes=[
             pltpu.VMEM((tensors, share, depth), BF16),
             pltpu.VMEM((depth, width), BF16),
+            pltpu.VMEM((width, depth), BF16),
             pltpu.VMEM((nch, SUB, width), BF16),
             pltpu.VMEM((nch, SUB, width), BF16),
             pltpu.VMEM((1, width), F32),
@@ -429,7 +434,7 @@
             dma, dma((max(chips - 1, 1), nch - 1 + count)),
             dma, dma, dma, dma((max(chips - 1, 1), 1 + count)),
             dma, dma, dma, dma, dma, dma, dma, dma,
-            pltpu.SemaphoreType.REGULAR((max(replicas // 2 - 1, 1) if reduce_dp else 1,)),
+            pltpu.SemaphoreType.REGULAR((max((replicas // 2 - 1).bit_length(), 1) if reduce_dp else 1,)),
         ],
         compiler_params=pltpu.CompilerParams(
             collective_id=0, has_side_effects=True, vmem_limit_bytes=VMEM_BYTES - spare),

time: 26.2 us -> 26 us (level)
  no operation moved by 1% of the time
where the time goes in v4:
time: 26 us; the launch traced here: 25.8 us
  Pallas kernels  25.2 us (97%)
  between operations  0.64 us (2%)
    pallas_call x1, Pallas kernels, body(): pl.pallas_call(functools.partial(kernel, reduce_dp, replicas, tensors), o...  24.1 us
    pallas_call x1, Pallas kernels, store(): pl.pallas_call(functools.partial(store_kernel, count), out_shape=tuple((j...  1.14 us

profile of v4, /device:TPU:0, one launch (start us, length us, event | category | flops | bytes accessed | tf_op | source)
XLA Modules:
  0.0 25.8 jit_solution(1743693433009759689)
XLA Ops:
  0.6 24.1 %shard_map.85 = (f32[32,640]{1,0:T(8,128)S(1)}, bf16[128,384]{1,0:T(8,128)(2,1)S(1)}, bf16[128,5120]{1,0:T(8,128)(2,1)S(1)}) custom-call(bf16[16,8,5120]{2,1,0:T(8,128)(2,1)} %bitcast.9, bf16[4,32,384]{2,1,0:T(8,128)(2,1)} %bitcast.11, bf16[384,5120]{1,0:T(8,128)(2,1)} %w_hbm.1, f32[1,5120]{1,0:T(1,128)} %bitcast.12, bf16[16,8,5120]{2,1,0:T(8,128)(2,1)} %bitcast.10, ...), custom_call_target="tpu_custom_call" | custom-call | tf_op jit(solution)/shard_map/pallas_call | solution.py:400
  24.7 1.1 %shard_map.86 = (f32[32,640]{1,0:T(8,128)}, bf16[128,384]{1,0:T(8,128)(2,1)}, bf16[128,5120]{1,0:T(8,128)(2,1)}) custom-call(f32[32,640]{1,0:T(8,128)S(1)} %get-tuple-element.9.refs_0_, bf16[128,384]{1,0:T(8,128)(2,1)S(1)} %get-tuple-element.10.refs_1_, bf16[128,5120]{1,0:T(8,128)(2,1)S(1)} %get-tuple-element.11.refs_2_), custom_call_target="tpu_custom_call" | custom-call | tf_op jit(solution)/shard_map/pallas_call | solution.py:372

commit v5 on v4

--- a/solution.py
+++ b/solution.py
@@ -25,6 +25,11 @@
     return 1
 
 
+def shares_of(block):
+    first = block // LANES // 2 * LANES
+    return (0, first), (first, block - first)
+
+
 def flipped(index, mask):
     bit = 1
     while bit <= mask:
@@ -49,7 +54,7 @@
            ctx, w, wt, res, cot, gain, slot_ref, lhs, psend, precv, own, ysend, yrecv,
            pick, pall, pat, gpick, glhs, graw, qsum, qsend, qrecv,
            load_sem, w_sem, p_send, p_recv, y_send, y_recv, a_send, a_recv, m_send, m_recv, f_send, f_recv,
-           c_send, c_recv, d_send, d_recv, r_send, r_recv, q_send, q_recv, ladder):
+           c_send, c_recv, d_send, d_recv, r_send, r_recv, q_send, q_recv, e_send, e_recv, ladder):
     rows, width = resid.shape
     chips = tensors // 2
     share = rows // tensors
@@ -97,20 +102,15 @@
                             device_id_type=MESH)
     greeted = tensors - 1
 
-    def greet(semaphore, reach):
+    def greet(semaphore, reach, cores=(tensor,)):
+        def tell_replica(replica):
+            for member in cores:
+                pl.semaphore_signal(semaphore, inc=1, device_id={"dp": replica, "tensor": member}, device_id_type=MESH)
+
         if reach == 1:
-            pl.semaphore_signal(semaphore, inc=1, device_id={"dp": dp + 1 - 2 * lax.rem(dp, 2), "tensor": tensor},
-                                device_id_type=MESH)
-
-        @pl.when(dp >= 2 * reach)
-        def _():
-            pl.semaphore_signal(semaphore, inc=1, device_id={"dp": dp - 2 * reach, "tensor": tensor},
-                                device_id_type=MESH)
-
-        @pl.when(dp + 2 * reach < replicas)
-        def _():
-            pl.semaphore_signal(semaphore, inc=1, device_id={"dp": dp + 2 * reach, "tensor": tensor},
-                                device_id_type=MESH)
+            tell_replica(dp + 1 - 2 * lax.rem(dp, 2))
+        pl.when(dp >= 2 * reach)(lambda: tell_replica(dp - 2 * reach))
+        pl.when(dp + 2 * reach < replicas)(lambda: tell_replica(dp + 2 * reach))
 
     def degree(reach):
         near = (dp >= 2 * reach).astype(jnp.int32) + (dp + 2 * reach < replicas).astype(jnp.int32)
@@ -120,8 +120,15 @@
     while reduce_dp and 2 ** len(reaches) < replicas // 2:
         reaches.append(2 ** len(reaches))
     if reduce_dp:
-        greet(barrier, 1)
-        greeted += degree(1)
+        greet(barrier, 1, (tensor, mate))
+        greeted += 2 * degree(1)
+
+    if reduce_dp:
+        narrow = shares_of(slots_out.shape[1])[0][1]
+
+        @pl.when(core == 0)
+        def _():
+            graw[:, :, narrow:] = jnp.zeros((graw.shape[0], SUB, graw.shape[2] - narrow), BF16)
 
     load_ctx.wait()
     for i in range(chips):
@@ -206,7 +213,7 @@
 
     def pass_pick(m):
         return pltpu.make_async_remote_copy(
-            src_ref=pat.at[tensor], dst_ref=gpick.at[m - 1], send_sem=d_send, recv_sem=d_recv,
+            src_ref=pat.at[tensor], dst_ref=gpick.at[m - 1, core], send_sem=d_send, recv_sem=d_recv,
             device_id={"dp": flipped(dp, m), "tensor": tensor}, device_id_type=MESH)
 
     if reduce_dp:
@@ -220,7 +227,7 @@
             table[g] = block
         turned = jnp.concatenate(table, axis=0).T.astype(BF16)
         pat[...] = turned.reshape(tensors, share, tensors * bucket)
-        gpick[replicas - 1] = pat[tensor]
+        gpick[replicas - 1, core] = pat[tensor]
         for turn in range(1, len(reaches)):
             climb(turn)
         for m in peers:
@@ -254,17 +261,36 @@
             src_ref=part, dst_ref=part, send_sem=f_send, recv_sem=f_recv.at[i, max(piece - last + 1, 0)],
             device_id={"dp": dp, "tensor": mate}, device_id_type=MESH)
 
-    block = graw.shape[2]
-
-    def columns(replica):
-        return pl.ds(pl.multiple_of(replica * block, LANES), block)
-
-    def spread(m, k):
+    block = slots_out.shape[1]
+    parts = shares_of(block)
+    wide = graw.shape[2]
+
+    def columns(replica, side):
+        return pl.ds(pl.multiple_of(replica * block + parts[side][0], LANES), parts[side][1])
+
+    def landing(m, k, side):
+        return graw.at[((m - 1) * 2 + core) * nch + k, :, pl.ds(0, parts[side][1])]
+
+    def spread(m, k, side):
         target = flipped(dp, m)
         return pltpu.make_async_remote_copy(
-            src_ref=resid.at[place_of(tensor, k), columns(target)], dst_ref=graw.at[(m - 1) * nch + k],
-            send_sem=r_send, recv_sem=r_recv,
-            device_id={"dp": target, "tensor": tensor}, device_id_type=MESH)
+            src_ref=resid.at[place_of(tensor, k), columns(target, side)], dst_ref=landing(m, k, side),
+            send_sem=r_send.at[side], recv_sem=r_recv, device_id={"dp": target, "tensor": chip * 2 + side},
+            device_id_type=MESH)
+
+    def keep(k):
+        for side in range(2):
+            @pl.when(core == side)
+            def _():
+                graw[((replicas - 1) * 2 + side) * nch + k, :, :parts[side][1]] = (
+                    resid[place_of(tensor, k), columns(dp, side)])
+
+            @pl.when(core != side)
+            def _():
+                pltpu.make_async_remote_copy(
+                    src_ref=resid.at[place_of(tensor, k), columns(dp, side)], dst_ref=landing(replicas, k, side),
+                    send_sem=r_send.at[side], recv_sem=r_recv, device_id={"dp": dp, "tensor": mate},
+                    device_id_type=MESH).start()
 
     for k in range(nch):
         hidden = own[far + k]
@@ -273,16 +299,17 @@
             hidden = hidden + yrecv[i * nch + k].astype(F32)
         resid[place_of(tensor, k)] = norm_backward(hidden, cot[k], gain[...])
         for m in peers:
-            spread(m, k).start()
+            for side in range(2):
+                spread(m, k, side).start()
         for i in range(chips - 1):
             for piece in (range(last, last + count) if k == last else (k,)):
                 gather(i, piece).start()
         beside(k).start()
+        if reduce_dp:
+            keep(k)
         for j in range(k * count // nch, (k + 1) * count // nch):
             span = pl.ds(j * cols, cols)
             wt[span] = w[:, span].T
-        if reduce_dp:
-            graw[(replicas - 1) * nch + k] = resid[place_of(tensor, k), columns(dp)]
 
     def rows_of(owner):
         return pl.ds(pl.multiple_of(owner * share, share), 2 * share)
@@ -296,6 +323,15 @@
             gather(i, piece).wait_recv()
             forward(i, piece).start()
 
+    def pass_on():
+        block = gpick.at[pl.ds(0, replicas), core]
+        return pltpu.make_async_remote_copy(
+            src_ref=block, dst_ref=block, send_sem=e_send, recv_sem=e_recv,
+            device_id={"dp": dp, "tensor": mate}, device_id_type=MESH)
+
+    if reduce_dp:
+        whole(gpick.at[pl.ds(0, replicas - 1), core], d_send, d_recv).wait_recv()
+        pass_on().start()
     if last:
         relay(0)
     whole(res, m_send, m_recv).wait_recv()
@@ -305,8 +341,8 @@
         back = back + backward(span, j)
     ctx_out[span] = back.astype(BF16)
     if reduce_dp:
-        whole(gpick.at[pl.ds(0, replicas - 1)], d_send, d_recv).wait_recv()
-        glhs[...] = gpick[...].reshape(replicas * share, tensors * bucket).astype(F32).T.astype(BF16)
+        whole(gpick.at[pl.ds(0, replicas), 1 - core], e_send, e_recv).wait_recv()
+        glhs[...] = gpick[...].reshape(2 * replicas * share, tensors * bucket).astype(F32).T.astype(BF16)
     for k in range(1, last):
         relay(k)
 
@@ -317,9 +353,13 @@
             device_id={"dp": dp, "tensor": target}, device_id_type=MESH)
 
     if reduce_dp:
-        whole(graw.at[pl.ds(0, (replicas - 1) * nch)], r_send, r_recv).wait_recv()
-        tokens = graw[...].astype(F32).reshape(replicas * share, block).astype(BF16)
-        gradient = jnp.dot(glhs[...], tokens, preferred_element_type=F32).reshape(tensors, bucket, block)
+        for side in range(2):
+            @pl.when(core == side)
+            def _():
+                whole(graw.at[pl.ds(0, (2 * replicas - 1) * nch), :, pl.ds(0, parts[side][1])],
+                      r_send.at[side], r_recv).wait_recv()
+        tokens = graw[...].astype(F32).reshape(2 * replicas * share, wide).astype(BF16)
+        gradient = jnp.dot(glhs[...], tokens, preferred_element_type=F32).reshape(tensors, bucket, wide)
         qsend[...] = gradient.astype(BF16)
         for i in others:
             settle(i).start()
@@ -349,13 +389,22 @@
     whole(res, m_send, m_recv).wait_send()
     if reduce_dp:
         whole(pall, c_send, c_recv).wait_send()
-        whole(gpick.at[pl.ds(0, replicas - 1)], d_send, d_recv).wait_send()
-        whole(graw.at[pl.ds(0, (replicas - 1) * nch)], r_send, r_recv).wait_send()
+        whole(gpick.at[pl.ds(0, replicas - 1), core], d_send, d_recv).wait_send()
+        pass_on().wait_send()
+        for side in range(2):
+            for sent, due in ((replicas - 1, core == side), (replicas, core != side)):
+                @pl.when(due)
+                def _():
+                    whole(graw.at[pl.ds(0, sent * nch), :, pl.ds(0, parts[side][1])],
+                          r_send.at[side], r_recv).wait_send()
         whole(qrecv, q_send, q_recv).wait_recv()
-        summed = qsum[tensor]
-        for i in others:
-            summed = summed + qrecv[i - 1].astype(F32)
-        slots_out[...] = summed * (1.0 / replicas)
+        same, cross = qsum[tensor], qrecv[0].astype(F32)
+        for i in range(2, tensors, 2):
+            same = same + qrecv[i - 1].astype(F32)
+            cross = cross + qrecv[i].astype(F32)
+        for side in range(2):
+            first, size = parts[side]
+            slots_out[:, first:first + size] = jnp.where(core == side, same, cross)[:, :size] * (1.0 / replicas)
         whole(qrecv, q_send, q_recv).wait_send()
 
 
@@ -391,9 +440,10 @@
     groups = chips * nch
     far = groups - nch
     count = pieces_of(width)
-    reduce_dp = (replicas > 1 and replicas & (replicas - 1) == 0 and width % (replicas * LANES) == 0
+    reduce_dp = (replicas > 1 and replicas & (replicas - 1) == 0 and width % (replicas * LANES) == 0 and width // replicas >= 2 * LANES
                  and rows == LANES and tensors * bucket == LANES)
     block = width // replicas if reduce_dp else LANES
+    wide = max(shares_of(block)[1][1], LANES)
     copies = replicas if reduce_dp else 1
     dma = pltpu.SemaphoreType.DMA
     spare = 4 * bucket * (block if reduce_dp else width) + 2 * rows * (depth + width)
@@ -423,17 +473,17 @@
             pltpu.VMEM((bucket, rows), BF16),
             pltpu.VMEM((tensors - 1, bucket, rows), BF16),
             pltpu.VMEM((tensors, share, tensors * bucket), BF16),
-            pltpu.VMEM((copies, share, tensors * bucket), BF16),
-            pltpu.VMEM((tensors * bucket, copies * share), BF16),
-            pltpu.VMEM((copies * nch, SUB, block), BF16),
-            pltpu.VMEM((tensors, bucket, block), F32),
-            pltpu.VMEM((tensors, bucket, block), BF16),
-            pltpu.VMEM((tensors - 1, bucket, block), BF16),
+            pltpu.VMEM((copies, 2, share, tensors * bucket), BF16),
+            pltpu.VMEM((tensors * bucket, 2 * copies * share), BF16),
+            pltpu.VMEM((2 * copies * nch, SUB, wide), BF16),
+            pltpu.VMEM((tensors, bucket, wide), F32),
+            pltpu.VMEM((tensors, bucket, wide), BF16),
+            pltpu.VMEM((tensors - 1, bucket, wide), BF16),
             dma((5,)), dma((count,)), dma, dma((count,)),
             dma, dma((max(chips - 1, 1), nch)),
             dma, dma((max(chips - 1, 1), nch - 1 + count)),
             dma, dma, dma, dma((max(chips - 1, 1), 1 + count)),
-            dma, dma, dma, dma, dma, dma, dma, dma,
+            dma, dma, dma, dma, dma((2,)), dma, dma, dma, dma, dma,
             pltpu.SemaphoreType.REGULAR((max((replicas // 2 - 1).bit_length(), 1) if reduce_dp else 1,)),
         ],
         compiler_params=pltpu.CompilerParams(

time: 26 us -> 25.8 us (level)
  no operation moved by 1% of the time
where the time goes in v5:
time: 25.8 us; the launch traced here: 25.7 us
  Pallas kernels  25 us (97%)
  between operations  0.64 us (2%)
    pallas_call x1, Pallas kernels, body(): pl.pallas_call(functools.partial(kernel, reduce_dp, replicas, tensors), o...  23.9 us
    pallas_call x1, Pallas kernels, store(): pl.pallas_call(functools.partial(store_kernel, count), out_shape=tuple((j...  1.14 us

profile of v5, /device:TPU:0, one launch (start us, length us, event | category | flops | bytes accessed | tf_op | source)
XLA Modules:
  0.0 25.7 jit_solution(542972783031159360)
XLA Ops:
  0.6 23.9 %shard_map.85 = (f32[32,640]{1,0:T(8,128)S(1)}, bf16[128,384]{1,0:T(8,128)(2,1)S(1)}, bf16[128,5120]{1,0:T(8,128)(2,1)S(1)}) custom-call(bf16[16,8,5120]{2,1,0:T(8,128)(2,1)} %bitcast.9, bf16[4,32,384]{2,1,0:T(8,128)(2,1)} %bitcast.11, bf16[384,5120]{1,0:T(8,128)(2,1)} %w_hbm.1, f32[1,5120]{1,0:T(1,128)} %bitcast.12, bf16[16,8,5120]{2,1,0:T(8,128)(2,1)} %bitcast.10, ...), custom_call_target="tpu_custom_call" | custom-call | tf_op jit(solution)/shard_map/pallas_call | solution.py:450
  24.5 1.1 %shard_map.86 = (f32[32,640]{1,0:T(8,128)}, bf16[128,384]{1,0:T(8,128)(2,1)}, bf16[128,5120]{1,0:T(8,128)(2,1)}) custom-call(f32[32,640]{1,0:T(8,128)S(1)} %get-tuple-element.9.refs_0_, bf16[128,384]{1,0:T(8,128)(2,1)S(1)} %get-tuple-element.10.refs_1_, bf16[128,5120]{1,0:T(8,128)(2,1)S(1)} %get-tuple-element.11.refs_2_), custom_call_target="tpu_custom_call" | custom-call | tf_op jit(solution)/shard_map/pallas_call | solution.py:421

commit v6 on v5

--- a/solution.py
+++ b/solution.py
@@ -199,7 +199,7 @@
         if j >= LAG:
             merge(j - LAG)
     for j in range(max(count - LAG, 0), count):
-        if j == count - 1:
+        if j == max(count - LAG, 0):
             climb(0)
         merge(j)
     for piece in range(count, total):
@@ -228,10 +228,14 @@
         turned = jnp.concatenate(table, axis=0).T.astype(BF16)
         pat[...] = turned.reshape(tensors, share, tensors * bucket)
         gpick[replicas - 1, core] = pat[tensor]
+        early = [m for m in (4, 3, 2, 1) if m in peers and reaches]
+        for m in early:
+            pass_pick(m).start()
         for turn in range(1, len(reaches)):
             climb(turn)
         for m in peers:
-            pass_pick(m).start()
+            if m not in early:
+                pass_pick(m).start()
 
     def place_of(owner, k):
         return pl.ds(pl.multiple_of((owner * nch + k) * SUB, SUB), SUB)
@@ -352,6 +356,9 @@
             src_ref=qsend.at[target], dst_ref=qrecv.at[i - 1], send_sem=q_send, recv_sem=q_recv,
             device_id={"dp": dp, "tensor": target}, device_id_type=MESH)
 
+    held = count - min(count, 3)
+    for j in range(count - held):
+        relay(last + j)
     if reduce_dp:
         for side in range(2):
             @pl.when(core == side)
@@ -364,7 +371,7 @@
         for i in others:
             settle(i).start()
         qsum[...] = gradient
-    for j in range(count):
+    for j in range(count - held, count):
         relay(last + j)
     backs = [None] * (chips - 1)
     for j in range(count):

time: 25.8 us -> 25.8 us (level)
  no operation moved by 1% of the time
where the time goes in v6:
time: 25.8 us; the launch traced here: 25.7 us
  Pallas kernels  25 us (97%)
  between operations  0.64 us (2%)
    pallas_call x1, Pallas kernels, body(): pl.pallas_call(functools.partial(kernel, reduce_dp, replicas, tensors), o...  23.9 us
    pallas_call x1, Pallas kernels, store(): pl.pallas_call(functools.partial(store_kernel, count), out_shape=tuple((j...  1.14 us

profile of v6, /device:TPU:0, one launch (start us, length us, event | category | flops | bytes accessed | tf_op | source)
XLA Modules:
  0.0 25.7 jit_solution(8526663193840772732)
XLA Ops:
  0.6 23.9 %shard_map.85 = (f32[32,640]{1,0:T(8,128)S(1)}, bf16[128,384]{1,0:T(8,128)(2,1)S(1)}, bf16[128,5120]{1,0:T(8,128)(2,1)S(1)}) custom-call(bf16[16,8,5120]{2,1,0:T(8,128)(2,1)} %bitcast.9, bf16[4,32,384]{2,1,0:T(8,128)(2,1)} %bitcast.11, bf16[384,5120]{1,0:T(8,128)(2,1)} %w_hbm.1, f32[1,5120]{1,0:T(1,128)} %bitcast.12, bf16[16,8,5120]{2,1,0:T(8,128)(2,1)} %bitcast.10, ...), custom_call_target="tpu_custom_call" | custom-call | tf_op jit(solution)/shard_map/pallas_call | solution.py:457
  24.5 1.1 %shard_map.86 = (f32[32,640]{1,0:T(8,128)}, bf16[128,384]{1,0:T(8,128)(2,1)}, bf16[128,5120]{1,0:T(8,128)(2,1)}) custom-call(f32[32,640]{1,0:T(8,128)S(1)} %get-tuple-element.9.refs_0_, bf16[128,384]{1,0:T(8,128)(2,1)S(1)} %get-tuple-element.10.refs_1_, bf16[128,5120]{1,0:T(8,128)(2,1)S(1)} %get-tuple-element.11.refs_2_), custom_call_target="tpu_custom_call" | custom-call | tf_op jit(solution)/shard_map/pallas_call | solution.py:428

commit v7 on v6

--- a/solution.py
+++ b/solution.py
@@ -39,22 +39,24 @@
     return index
 
 
-def norm_backward(hidden, cot_rows, gain):
+def centered(values):
+    return values - jnp.sum(values, axis=-1, keepdims=True) * (1.0 / values.shape[-1])
+
+
+def norm_backward(hidden, lift):
     scale = 1.0 / hidden.shape[-1]
-    center = hidden - jnp.sum(hidden, axis=-1, keepdims=True) * scale
+    center = centered(hidden)
     inverse = lax.rsqrt(jnp.sum(center * center, axis=-1, keepdims=True) * scale + 1e-05)
-    upstream = cot_rows.astype(F32) * gain
-    mean_up = jnp.sum(upstream, axis=-1, keepdims=True) * scale
-    slope = jnp.sum(upstream * center, axis=-1, keepdims=True) * scale * inverse * inverse
-    return (inverse * (upstream - mean_up - center * slope)).astype(BF16)
+    slope = jnp.sum(lift * center, axis=-1, keepdims=True) * scale * inverse * inverse
+    return (inverse * (lift - center * slope)).astype(BF16)
 
 
 def kernel(reduce_dp, replicas, tensors, res_hbm, ctx_hbm, w_hbm, gain_hbm, cot_hbm, slot_hbm,
            slots_out, ctx_out, resid,
-           ctx, w, wt, res, cot, gain, slot_ref, lhs, psend, precv, own, ysend, yrecv,
+           ctx, w, wt, res, cot, lift, gain, slot_ref, lhs, psend, precv, own, ysend, yrecv,
            pick, pall, pat, gpick, glhs, graw, qsum, qsend, qrecv,
-           load_sem, w_sem, p_send, p_recv, y_send, y_recv, a_send, a_recv, m_send, m_recv, f_send, f_recv,
-           c_send, c_recv, d_send, d_recv, r_send, r_recv, q_send, q_recv, e_send, e_recv, ladder):
+           load_sem, w_sem, p_recv, y_recv, a_recv, m_recv, f_recv, c_recv, d_recv, e_recv, r_recv, q_recv,
+           s_send, t_send, r_send, q_send, ladder):
     rows, width = resid.shape
     chips = tensors // 2
     share = rows // tensors
@@ -123,27 +125,26 @@
         greet(barrier, 1, (tensor, mate))
         greeted += 2 * degree(1)
 
-    if reduce_dp:
-        narrow = shares_of(slots_out.shape[1])[0][1]
-
-        @pl.when(core == 0)
-        def _():
-            graw[:, :, narrow:] = jnp.zeros((graw.shape[0], SUB, graw.shape[2] - narrow), BF16)
-
+    load_slot.wait()
+    square = (bucket, bucket)
+    diagonal = lax.broadcasted_iota(jnp.int32, square, 0) == lax.broadcasted_iota(jnp.int32, square, 1)
+    order = jnp.sum(jnp.where(diagonal, slot_ref[...].astype(F32), 0.0), axis=1, keepdims=True)
+    place = lax.broadcasted_iota(jnp.int32, (bucket, depth), 1).astype(F32)
+    chosen = jnp.where(place == order, 1.0, 0.0).astype(BF16)
     load_ctx.wait()
     for i in range(chips):
         lhs[pl.ds(i * share, share)] = ctx[ahead(i) * 2 + (1 - core)]
         lhs[pl.ds((chips + i) * share, share)] = ctx[ahead(i) * 2 + core]
 
     def to_mate(j):
-        span = pl.ds(j * cols, cols)
-        return pltpu.make_async_remote_copy(
-            src_ref=psend.at[:, :, span], dst_ref=precv.at[:, :, span], send_sem=p_send, recv_sem=p_recv.at[j],
+        part, span = (pl.ds(0, far), pl.ds(j * cols, cols)) if j < count else (pl.ds(far, nch), pl.ds(0, width))
+        return pltpu.make_async_remote_copy(
+            src_ref=psend.at[part, :, span], dst_ref=precv.at[part, :, span], send_sem=s_send, recv_sem=p_recv.at[j],
             device_id={"dp": dp, "tensor": mate}, device_id_type=MESH)
 
     def tell(i):
         return pltpu.make_async_remote_copy(
-            src_ref=pick, dst_ref=pall.at[i - 1], send_sem=c_send, recv_sem=c_recv,
+            src_ref=pick, dst_ref=pall.at[i - 1], send_sem=t_send, recv_sem=c_recv,
             device_id={"dp": dp, "tensor": lax.rem(tensor + i, tensors)}, device_id_type=MESH)
 
     def across(i, piece):
@@ -152,7 +153,7 @@
         else:
             src, dst = (ref.at[i * nch + piece - count + 1] for ref in (ysend, yrecv))
         return pltpu.make_async_remote_copy(
-            src_ref=src, dst_ref=dst, send_sem=y_send, recv_sem=y_recv.at[i, max(piece - count + 1, 0)],
+            src_ref=src, dst_ref=dst, send_sem=s_send, recv_sem=y_recv.at[i, max(piece - count + 1, 0)],
             device_id={"dp": dp, "tensor": ahead(i) * 2 + core}, device_id_type=MESH)
 
     def merge(j):
@@ -168,10 +169,13 @@
         if turn + 1 < len(reaches):
             greet(ladder.at[turn + 1], reaches[turn + 1])
 
-    def whole(ref, send, recv):
-        return pltpu.make_async_remote_copy(
-            src_ref=ref, dst_ref=ref, send_sem=send, recv_sem=recv,
+    def whole(ref, semaphore):
+        return pltpu.make_async_remote_copy(
+            src_ref=ref, dst_ref=ref, send_sem=semaphore, recv_sem=semaphore,
             device_id={"dp": dp, "tensor": mate}, device_id_type=MESH)
+
+    def sized(height, breadth):
+        return w.at[pl.ds(0, height), pl.ds(0, breadth)]
 
     total = count + nch - 1
     for j in range(count):
@@ -181,12 +185,6 @@
         psend[:, :, span] = product[:groups].astype(BF16)
         own[:, :, span] = product[groups:]
         if j == 0:
-            load_slot.wait()
-            square = (bucket, bucket)
-            diagonal = lax.broadcasted_iota(jnp.int32, square, 0) == lax.broadcasted_iota(jnp.int32, square, 1)
-            order = jnp.sum(jnp.where(diagonal, slot_ref[...].astype(F32), 0.0), axis=1, keepdims=True)
-            place = lax.broadcasted_iota(jnp.int32, (bucket, depth), 1).astype(F32)
-            chosen = jnp.where(place == order, 1.0, 0.0).astype(BF16)
             pick[...] = lax.dot_general(chosen, ctx[...].reshape(rows, depth), (((1,), (1,)), ((), ())),
                                         preferred_element_type=F32).astype(BF16)
             pl.semaphore_wait(barrier, greeted)
@@ -198,6 +196,7 @@
                 tell(i).start()
         if j >= LAG:
             merge(j - LAG)
+    to_mate(count).start()
     for j in range(max(count - LAG, 0), count):
         if j == max(count - LAG, 0):
             climb(0)
@@ -208,25 +207,27 @@
 
     for copy in load_rest:
         copy.wait()
+    to_mate(count).wait_recv()
     for k in range(nch):
         own[far + k] = own[far + k] + precv[far + k].astype(F32) + res[k].astype(F32)
+        lift[k] = centered(cot[k].astype(F32) * gain[...])
 
     def pass_pick(m):
         return pltpu.make_async_remote_copy(
-            src_ref=pat.at[tensor], dst_ref=gpick.at[m - 1, core], send_sem=d_send, recv_sem=d_recv,
+            src_ref=pat.at[tensor], dst_ref=gpick.at[m - 1, core], send_sem=t_send, recv_sem=d_recv,
             device_id={"dp": flipped(dp, m), "tensor": tensor}, device_id_type=MESH)
 
     if reduce_dp:
         table = [None] * tensors
-        whole(pall, c_send, c_recv).wait_recv()
+        whole(pall, c_recv).wait_recv()
         for g in range(tensors):
             offset = lax.rem(tensor - g + tensors, tensors)
             block = pick[...].astype(F32)
             for i in others:
                 block = jnp.where(offset == i, pall[i - 1].astype(F32), block)
             table[g] = block
-        turned = jnp.concatenate(table, axis=0).T.astype(BF16)
-        pat[...] = turned.reshape(tensors, share, tensors * bucket)
+        turned = jnp.concatenate(table, axis=0).T
+        pat[...] = turned.reshape(tensors, nch, SUB, tensors * bucket).astype(BF16)
         gpick[replicas - 1, core] = pat[tensor]
         early = [m for m in (4, 3, 2, 1) if m in peers and reaches]
         for m in early:
@@ -241,72 +242,75 @@
         return pl.ds(pl.multiple_of((owner * nch + k) * SUB, SUB), SUB)
 
     last = nch - 1
+    edges = sorted({0, count * 2 // 5, count * 4 // 5, count})
+    slices = list(zip(edges, edges[1:]))
 
     def part_of(owner, piece):
         if piece < last:
             return resid.at[place_of(owner, piece)]
-        return resid.at[place_of(owner, last), pl.ds((piece - last) * cols, cols)]
+        first, end = slices[piece - last]
+        return resid.at[place_of(owner, last), pl.ds(first * cols, (end - first) * cols)]
 
     def gather(i, piece):
         part = part_of(tensor, piece)
         return pltpu.make_async_remote_copy(
-            src_ref=part, dst_ref=part, send_sem=a_send, recv_sem=a_recv.at[i, piece],
+            src_ref=part, dst_ref=part, send_sem=s_send, recv_sem=a_recv.at[i, piece],
             device_id={"dp": dp, "tensor": ahead(i) * 2 + core}, device_id_type=MESH)
 
     def beside(k):
         span = place_of(tensor, k)
         return pltpu.make_async_remote_copy(
-            src_ref=resid.at[span], dst_ref=resid.at[span], send_sem=m_send, recv_sem=m_recv,
+            src_ref=resid.at[span], dst_ref=resid.at[span], send_sem=s_send, recv_sem=m_recv,
             device_id={"dp": dp, "tensor": mate}, device_id_type=MESH)
 
     def forward(i, piece):
         part = part_of(behind(i) * 2 + core, piece)
         return pltpu.make_async_remote_copy(
-            src_ref=part, dst_ref=part, send_sem=f_send, recv_sem=f_recv.at[i, max(piece - last + 1, 0)],
+            src_ref=part, dst_ref=part, send_sem=s_send, recv_sem=f_recv.at[i, max(piece - last + 1, 0)],
             device_id={"dp": dp, "tensor": mate}, device_id_type=MESH)
 
     block = slots_out.shape[1]
     parts = shares_of(block)
-    wide = graw.shape[2]
+    wide = graw.shape[3]
 
     def columns(replica, side):
         return pl.ds(pl.multiple_of(replica * block + parts[side][0], LANES), parts[side][1])
 
     def landing(m, k, side):
-        return graw.at[((m - 1) * 2 + core) * nch + k, :, pl.ds(0, parts[side][1])]
+        return graw.at[k, (m - 1) * 2 + core, :, pl.ds(0, parts[side][1])]
 
     def spread(m, k, side):
         target = flipped(dp, m)
         return pltpu.make_async_remote_copy(
             src_ref=resid.at[place_of(tensor, k), columns(target, side)], dst_ref=landing(m, k, side),
-            send_sem=r_send.at[side], recv_sem=r_recv, device_id={"dp": target, "tensor": chip * 2 + side},
-            device_id_type=MESH)
+            send_sem=r_send.at[side], recv_sem=r_recv.at[int(k == last)],
+            device_id={"dp": target, "tensor": chip * 2 + side}, device_id_type=MESH)
 
     def keep(k):
         for side in range(2):
             @pl.when(core == side)
             def _():
-                graw[((replicas - 1) * 2 + side) * nch + k, :, :parts[side][1]] = (
+                graw[k, (replicas - 1) * 2 + side, :, :parts[side][1]] = (
                     resid[place_of(tensor, k), columns(dp, side)])
 
             @pl.when(core != side)
             def _():
                 pltpu.make_async_remote_copy(
                     src_ref=resid.at[place_of(tensor, k), columns(dp, side)], dst_ref=landing(replicas, k, side),
-                    send_sem=r_send.at[side], recv_sem=r_recv, device_id={"dp": dp, "tensor": mate},
-                    device_id_type=MESH).start()
+                    send_sem=r_send.at[side], recv_sem=r_recv.at[int(k == last)],
+                    device_id={"dp": dp, "tensor": mate}, device_id_type=MESH).start()
 
     for k in range(nch):
         hidden = own[far + k]
         for i in range(chips - 1):
-            whole(yrecv.at[i * nch + k], y_send, y_recv.at[i, k]).wait_recv()
+            whole(yrecv.at[i * nch + k], y_recv.at[i, k]).wait_recv()
             hidden = hidden + yrecv[i * nch + k].astype(F32)
-        resid[place_of(tensor, k)] = norm_backward(hidden, cot[k], gain[...])
+        resid[place_of(tensor, k)] = norm_backward(hidden, lift[k])
         for m in peers:
             for side in range(2):
                 spread(m, k, side).start()
         for i in range(chips - 1):
-            for piece in (range(last, last + count) if k == last else (k,)):
+            for piece in (range(last, last + len(slices)) if k == last else (k,)):
                 gather(i, piece).start()
         beside(k).start()
         if reduce_dp:
@@ -327,60 +331,75 @@
             gather(i, piece).wait_recv()
             forward(i, piece).start()
 
+    half_k = 2 * replicas * SUB
+
     def pass_on():
         block = gpick.at[pl.ds(0, replicas), core]
         return pltpu.make_async_remote_copy(
-            src_ref=block, dst_ref=block, send_sem=e_send, recv_sem=e_recv,
+            src_ref=block, dst_ref=block, send_sem=t_send, recv_sem=e_recv,
             device_id={"dp": dp, "tensor": mate}, device_id_type=MESH)
 
     if reduce_dp:
-        whole(gpick.at[pl.ds(0, replicas - 1), core], d_send, d_recv).wait_recv()
+        whole(gpick.at[pl.ds(0, replicas - 1), core], d_recv).wait_recv()
         pass_on().start()
     if last:
         relay(0)
-    whole(res, m_send, m_recv).wait_recv()
+    whole(res, m_recv).wait_recv()
     span = rows_of(chip * 2)
     back = backward(span, 0)
     for j in range(1, count):
         back = back + backward(span, j)
     ctx_out[span] = back.astype(BF16)
     if reduce_dp:
-        whole(gpick.at[pl.ds(0, replicas), 1 - core], e_send, e_recv).wait_recv()
-        glhs[...] = gpick[...].reshape(2 * replicas * share, tensors * bucket).astype(F32).T.astype(BF16)
+        whole(gpick.at[pl.ds(0, replicas), 1 - core], e_recv).wait_recv()
+        for k in range(nch):
+            block = gpick[:, :, k].astype(F32).reshape(half_k, tensors * bucket)
+            glhs[:, k * half_k:(k + 1) * half_k] = block.T.astype(BF16)
     for k in range(1, last):
         relay(k)
 
-    def settle(i):
-        target = lax.rem(tensor + i, tensors)
-        return pltpu.make_async_remote_copy(
-            src_ref=qsend.at[target], dst_ref=qrecv.at[i - 1], send_sem=q_send, recv_sem=q_recv,
-            device_id={"dp": dp, "tensor": target}, device_id_type=MESH)
-
-    held = count - min(count, 3)
-    for j in range(count - held):
-        relay(last + j)
-    if reduce_dp:
+    def received(first, chunks, turn):
         for side in range(2):
             @pl.when(core == side)
             def _():
-                whole(graw.at[pl.ds(0, (2 * replicas - 1) * nch), :, pl.ds(0, parts[side][1])],
-                      r_send.at[side], r_recv).wait_recv()
-        tokens = graw[...].astype(F32).reshape(2 * replicas * share, wide).astype(BF16)
-        gradient = jnp.dot(glhs[...], tokens, preferred_element_type=F32).reshape(tensors, bucket, wide)
+                whole(graw.at[pl.ds(first, chunks), pl.ds(0, 2 * replicas - 1), :, pl.ds(0, parts[side][1])],
+                      r_recv.at[turn]).wait_recv()
+        tokens = graw[pl.ds(first, chunks)].astype(F32).reshape(chunks * half_k, wide).astype(BF16)
+        picked = glhs[:, first * half_k:(first + chunks) * half_k]
+        return jnp.dot(picked, tokens, preferred_element_type=F32).reshape(tensors, bucket, wide)
+
+    def settle(i, side):
+        target = lax.rem(tensor + i, tensors)
+        span = pl.ds(0, parts[side][1])
+        return pltpu.make_async_remote_copy(
+            src_ref=qsend.at[target, :, span], dst_ref=qrecv.at[i - 1, :, span], send_sem=q_send, recv_sem=q_recv,
+            device_id={"dp": dp, "tensor": target}, device_id_type=MESH)
+
+    if reduce_dp and last:
+        qsum[...] = received(0, last, 0)
+    relay(last)
+    if reduce_dp:
+        gradient = received(last, 1, 1)
+        if last:
+            gradient = gradient + qsum[...]
         qsend[...] = gradient.astype(BF16)
-        for i in others:
-            settle(i).start()
+        for side in range(2):
+            @pl.when(core == side)
+            def _():
+                for i in others:
+                    settle(i, side).start()
         qsum[...] = gradient
-    for j in range(count - held, count):
-        relay(last + j)
+    for piece in range(1, len(slices)):
+        relay(last + piece)
     backs = [None] * (chips - 1)
-    for j in range(count):
+    for piece, (first, end) in enumerate(slices):
         for i in range(chips - 1):
-            if j == 0 and last:
-                whole(ysend.at[pl.ds(0, last)], f_send, f_recv.at[i, 0]).wait_recv()
-            forward(i, last + j).wait_recv()
-            term = backward(rows_of(behind(i) * 2), j)
-            backs[i] = term if j == 0 else backs[i] + term
+            if piece == 0 and last:
+                whole(ysend.at[pl.ds(0, last)], f_recv.at[i, 0]).wait_recv()
+            forward(i, last + piece).wait_recv()
+            for j in range(first, end):
+                term = backward(rows_of(behind(i) * 2), j)
+                backs[i] = term if backs[i] is None else backs[i] + term
     for i in range(chips - 1):
         ctx_out[rows_of(behind(i) * 2)] = backs[i].astype(BF16)
 
@@ -389,30 +408,28 @@
             span = pl.ds(j * cols, cols)
             slots_out[:, span] = jnp.dot(pick[...], resid[:, span], preferred_element_type=F32)
 
-    whole(psend, p_send, p_recv.at[0]).wait_send()
-    if far:
-        for semaphore in (y_send, a_send, f_send):
-            whole(ysend, semaphore, m_recv).wait_send()
-    whole(res, m_send, m_recv).wait_send()
+    whole(sized((groups + 3 * far + nch) * SUB, width), s_send).wait_send()
     if reduce_dp:
-        whole(pall, c_send, c_recv).wait_send()
-        whole(gpick.at[pl.ds(0, replicas - 1), core], d_send, d_recv).wait_send()
-        pass_on().wait_send()
+        small = (tensors - 1) * bucket + (2 * replicas - 1) * share
+        whole(sized(small // 4, 4 * LANES), t_send).wait_send()
         for side in range(2):
             for sent, due in ((replicas - 1, core == side), (replicas, core != side)):
                 @pl.when(due)
                 def _():
-                    whole(graw.at[pl.ds(0, sent * nch), :, pl.ds(0, parts[side][1])],
-                          r_send.at[side], r_recv).wait_send()
-        whole(qrecv, q_send, q_recv).wait_recv()
-        same, cross = qsum[tensor], qrecv[0].astype(F32)
-        for i in range(2, tensors, 2):
-            same = same + qrecv[i - 1].astype(F32)
-            cross = cross + qrecv[i].astype(F32)
+                    whole(graw.at[:, pl.ds(0, sent), :, pl.ds(0, parts[side][1])], r_send.at[side]).wait_send()
+
+            @pl.when(core == side)
+            def _():
+                mine, theirs = parts[side][1], parts[1 - side][1]
+                whole(sized(bucket, (tensors - 1) * mine), q_send).wait_send()
+                whole(sized(bucket, (tensors // 2 - 1) * mine + tensors // 2 * theirs), q_recv).wait_recv()
         for side in range(2):
             first, size = parts[side]
-            slots_out[:, first:first + size] = jnp.where(core == side, same, cross)[:, :size] * (1.0 / replicas)
-        whole(qrecv, q_send, q_recv).wait_send()
+            same, cross = qsum[tensor][:, :size], qrecv[0, :, :size].astype(F32)
+            for i in range(2, tensors, 2):
+                same = same + qrecv[i - 1, :, :size].astype(F32)
+                cross = cross + qrecv[i, :, :size].astype(F32)
+            slots_out[:, first:first + size] = jnp.where(core == side, same, cross) * (1.0 / replicas)
 
 
 def store_kernel(count, *refs):
@@ -469,6 +486,7 @@
             pltpu.VMEM((width, depth), BF16),
             pltpu.VMEM((nch, SUB, width), BF16),
             pltpu.VMEM((nch, SUB, width), BF16),
+            pltpu.VMEM((nch, SUB, width), F32),
             pltpu.VMEM((1, width), F32),
             pltpu.VMEM((1, bucket), jnp.int32),
             pltpu.VMEM((rows, depth), BF16),
@@ -479,18 +497,17 @@
             pltpu.VMEM((max(far, 1), SUB, width), BF16),
             pltpu.VMEM((bucket, rows), BF16),
             pltpu.VMEM((tensors - 1, bucket, rows), BF16),
-            pltpu.VMEM((tensors, share, tensors * bucket), BF16),
-            pltpu.VMEM((copies, 2, share, tensors * bucket), BF16),
+            pltpu.VMEM((tensors, nch, SUB, tensors * bucket), BF16),
+            pltpu.VMEM((copies, 2, nch, SUB, tensors * bucket), BF16),
             pltpu.VMEM((tensors * bucket, 2 * copies * share), BF16),
-            pltpu.VMEM((2 * copies * nch, SUB, wide), BF16),
+            pltpu.VMEM((nch, 2 * copies, SUB, wide), BF16),
             pltpu.VMEM((tensors, bucket, wide), F32),
             pltpu.VMEM((tensors, bucket, wide), BF16),
             pltpu.VMEM((tensors - 1, bucket, wide), BF16),
-            dma((5,)), dma((count,)), dma, dma((count,)),
-            dma, dma((max(chips - 1, 1), nch)),
-            dma, dma((max(chips - 1, 1), nch - 1 + count)),
-            dma, dma, dma, dma((max(chips - 1, 1), 1 + count)),
-            dma, dma, dma, dma, dma((2,)), dma, dma, dma, dma, dma,
+            dma((5,)), dma((count,)), dma((count + 1,)), dma((chips - 1, nch)),
+            dma((chips - 1, nch + 2)), dma, dma((chips - 1, 4)),
+            dma, dma, dma, dma((2,)), dma,
+            dma, dma, dma((2,)), dma,
             pltpu.SemaphoreType.REGULAR((max((replicas // 2 - 1).bit_length(), 1) if reduce_dp else 1,)),
         ],
         compiler_params=pltpu.CompilerParams(

time: 25.8 us -> 25.3 us (0.981)
  Pallas kernels: 25 us -> 24.4 us
    pallas_call x1, Pallas kernels: 23.9 us -> 23.3 us  [body(): pl.pallas_call(functools.partial(kernel, reduce_dp, replicas, tensors), o...]
where the time goes in v7:
time: 25.3 us; the launch traced here: 25.1 us
  Pallas kernels  24.4 us (96%)
  between operations  0.64 us (3%)
    pallas_call x1, Pallas kernels, body(): pl.pallas_call(functools.partial(kernel, reduce_dp, replicas, tensors), o...  23.3 us
    pallas_call x1, Pallas kernels, store(): pl.pallas_call(functools.partial(store_kernel, count), out_shape=tuple((j...  1.14 us

profile of v7, /device:TPU:0, one launch (start us, length us, event | category | flops | bytes accessed | tf_op | source)
XLA Modules:
  0.0 25.1 jit_solution(11933498749471884721)
XLA Ops:
  0.6 23.3 %shard_map.85 = (f32[32,640]{1,0:T(8,128)S(1)}, bf16[128,384]{1,0:T(8,128)(2,1)S(1)}, bf16[128,5120]{1,0:T(8,128)(2,1)S(1)}) custom-call(bf16[16,8,5120]{2,1,0:T(8,128)(2,1)} %bitcast.9, bf16[4,32,384]{2,1,0:T(8,128)(2,1)} %bitcast.11, bf16[384,5120]{1,0:T(8,128)(2,1)} %w_hbm.1, f32[1,5120]{1,0:T(1,128)} %bitcast.12, bf16[16,8,5120]{2,1,0:T(8,128)(2,1)} %bitcast.10, ...), custom_call_target="tpu_custom_call" | custom-call | tf_op jit(solution)/shard_map/pallas_call | solution.py:474
  23.9 1.1 %shard_map.86 = (f32[32,640]{1,0:T(8,128)}, bf16[128,384]{1,0:T(8,128)(2,1)}, bf16[128,5120]{1,0:T(8,128)(2,1)}) custom-call(f32[32,640]{1,0:T(8,128)S(1)} %get-tuple-element.9.refs_0_, bf16[128,384]{1,0:T(8,128)(2,1)S(1)} %get-tuple-element.10.refs_1_, bf16[128,5120]{1,0:T(8,128)(2,1)S(1)} %get-tuple-element.11.refs_2_), custom_call_target="tpu_custom_call" | custom-call | tf_op jit(solution)/shard_map/pallas_call | solution.py:445

commit v8 on v7

--- a/solution.py
+++ b/solution.py
@@ -53,10 +53,10 @@
 
 def kernel(reduce_dp, replicas, tensors, res_hbm, ctx_hbm, w_hbm, gain_hbm, cot_hbm, slot_hbm,
            slots_out, ctx_out, resid,
-           ctx, w, wt, res, cot, lift, gain, slot_ref, lhs, psend, precv, own, ysend, yrecv,
+           ctx, w, wt, res, cot, lift, gain, slot_ref, lhs, psend, precv, own, ysend, yrecv, yextra,
            pick, pall, pat, gpick, glhs, graw, qsum, qsend, qrecv,
            load_sem, w_sem, p_recv, y_recv, a_recv, m_recv, f_recv, c_recv, d_recv, e_recv, r_recv, q_recv,
-           s_send, t_send, r_send, q_send, ladder):
+           s_send, t_send, r_send, q_send, x_send, x_recv, ladder):
     rows, width = resid.shape
     chips = tensors // 2
     share = rows // tensors
@@ -147,21 +147,27 @@
             src_ref=pick, dst_ref=pall.at[i - 1], send_sem=t_send, recv_sem=c_recv,
             device_id={"dp": dp, "tensor": lax.rem(tensor + i, tensors)}, device_id_type=MESH)
 
-    def across(i, piece):
-        if piece < count:
-            src, dst = (ref.at[i * nch, :, pl.ds(piece * cols, cols)] for ref in (ysend, yrecv))
-        else:
-            src, dst = (ref.at[i * nch + piece - count + 1] for ref in (ysend, yrecv))
-        return pltpu.make_async_remote_copy(
-            src_ref=src, dst_ref=dst, send_sem=s_send, recv_sem=y_recv.at[i, max(piece - count + 1, 0)],
+    def across(i, k, first=0, pieces=count):
+        src, dst = (ref.at[i * nch + k, :, pl.ds(first * cols, pieces * cols)] for ref in (ysend, yrecv))
+        return pltpu.make_async_remote_copy(
+            src_ref=src, dst_ref=dst, send_sem=s_send, recv_sem=y_recv.at[i, k],
             device_id={"dp": dp, "tensor": ahead(i) * 2 + core}, device_id_type=MESH)
+
+    def unmerged(i):
+        return pltpu.make_async_remote_copy(
+            src_ref=psend.at[i * nch, :, pl.ds(0, cols)], dst_ref=yextra.at[i], send_sem=x_send, recv_sem=x_recv,
+            device_id={"dp": dp, "tensor": ahead(i) * 2 + (1 - core)}, device_id_type=MESH)
 
     def merge(j):
         span = pl.ds(j * cols, cols)
         to_mate(j).wait_recv()
-        ysend[:, :, span] = (own[:far, :, span] + precv[:far, :, span].astype(F32)).astype(BF16)
         for i in range(chips - 1):
-            across(i, j).start()
+            part = pl.ds(i * nch + int(j == 0), nch - int(j == 0))
+            ysend[part, :, span] = (own[part, :, span] + precv[part, :, span].astype(F32)).astype(BF16)
+            if j > 0:
+                across(i, 0, j, 1).start()
+            else:
+                across(i, 1, 0, 1).start()
 
     def climb(turn):
         if turn < len(reaches):
@@ -177,7 +183,6 @@
     def sized(height, breadth):
         return w.at[pl.ds(0, height), pl.ds(0, breadth)]
 
-    total = count + nch - 1
     for j in range(count):
         span = pl.ds(j * cols, cols)
         loads_w[j].wait()
@@ -190,6 +195,10 @@
             pl.semaphore_wait(barrier, greeted)
         to_mate(j).start()
         if j == 0:
+            for i in range(chips - 1):
+                ysend[i * nch, :, span] = own[i * nch, :, span].astype(BF16)
+                across(i, 0, 0, 1).start()
+                unmerged(i).start()
             if reaches:
                 greet(ladder.at[0], 1)
             for i in others:
@@ -201,13 +210,19 @@
         if j == max(count - LAG, 0):
             climb(0)
         merge(j)
-    for piece in range(count, total):
+    for k in range(1, nch):
         for i in range(chips - 1):
-            across(i, piece).start()
+            if k == 1:
+                across(i, k, 1, count - 1).start()
+            else:
+                across(i, k).start()
 
     for copy in load_rest:
         copy.wait()
     to_mate(count).wait_recv()
+    whole(yextra, x_recv).wait_recv()
+    for i in range(chips - 1):
+        own[far, :, :cols] = own[far, :, :cols] + yextra[i].astype(F32)
     for k in range(nch):
         own[far + k] = own[far + k] + precv[far + k].astype(F32) + res[k].astype(F32)
         lift[k] = centered(cot[k].astype(F32) * gain[...])
@@ -254,7 +269,7 @@
     def gather(i, piece):
         part = part_of(tensor, piece)
         return pltpu.make_async_remote_copy(
-            src_ref=part, dst_ref=part, send_sem=s_send, recv_sem=a_recv.at[i, piece],
+            src_ref=part, dst_ref=part, send_sem=s_send, recv_sem=a_recv.at[i, max(piece - last + 1, 0)],
             device_id={"dp": dp, "tensor": ahead(i) * 2 + core}, device_id_type=MESH)
 
     def beside(k):
@@ -264,9 +279,13 @@
             device_id={"dp": dp, "tensor": mate}, device_id_type=MESH)
 
     def forward(i, piece):
-        part = part_of(behind(i) * 2 + core, piece)
-        return pltpu.make_async_remote_copy(
-            src_ref=part, dst_ref=part, send_sem=s_send, recv_sem=f_recv.at[i, max(piece - last + 1, 0)],
+        owner = behind(i) * 2 + core
+        if piece < 0:
+            part = resid.at[pl.ds(pl.multiple_of(owner * share, share), last * SUB)]
+        else:
+            part = part_of(owner, last + piece)
+        return pltpu.make_async_remote_copy(
+            src_ref=part, dst_ref=part, send_sem=s_send, recv_sem=f_recv.at[i, piece + 1],
             device_id={"dp": dp, "tensor": mate}, device_id_type=MESH)
 
     block = slots_out.shape[1]
@@ -328,7 +347,10 @@
 
     def relay(piece):
         for i in range(chips - 1):
-            gather(i, piece).wait_recv()
+            if piece < 0:
+                whole(ysend.at[pl.ds(0, last)], a_recv.at[i, 0]).wait_recv()
+            else:
+                gather(i, last + piece).wait_recv()
             forward(i, piece).start()
 
     half_k = 2 * replicas * SUB
@@ -342,8 +364,6 @@
     if reduce_dp:
         whole(gpick.at[pl.ds(0, replicas - 1), core], d_recv).wait_recv()
         pass_on().start()
-    if last:
-        relay(0)
     whole(res, m_recv).wait_recv()
     span = rows_of(chip * 2)
     back = backward(span, 0)
@@ -355,8 +375,7 @@
         for k in range(nch):
             block = gpick[:, :, k].astype(F32).reshape(half_k, tensors * bucket)
             glhs[:, k * half_k:(k + 1) * half_k] = block.T.astype(BF16)
-    for k in range(1, last):
-        relay(k)
+    relay(-1)
 
     def received(first, chunks, turn):
         for side in range(2):
@@ -377,7 +396,7 @@
 
     if reduce_dp and last:
         qsum[...] = received(0, last, 0)
-    relay(last)
+    relay(0)
     if reduce_dp:
         gradient = received(last, 1, 1)
         if last:
@@ -390,13 +409,13 @@
                     settle(i, side).start()
         qsum[...] = gradient
     for piece in range(1, len(slices)):
-        relay(last + piece)
+        relay(piece)
     backs = [None] * (chips - 1)
     for piece, (first, end) in enumerate(slices):
         for i in range(chips - 1):
-            if piece == 0 and last:
-                whole(ysend.at[pl.ds(0, last)], f_recv.at[i, 0]).wait_recv()
-            forward(i, last + piece).wait_recv()
+            if piece == 0:
+                forward(i, -1).wait_recv()
+            forward(i, piece).wait_recv()
             for j in range(first, end):
                 term = backward(rows_of(behind(i) * 2), j)
                 backs[i] = term if backs[i] is None else backs[i] + term
@@ -409,6 +428,7 @@
             slots_out[:, span] = jnp.dot(pick[...], resid[:, span], preferred_element_type=F32)
 
     whole(sized((groups + 3 * far + nch) * SUB, width), s_send).wait_send()
+    whole(yextra, x_send).wait_send()
     if reduce_dp:
         small = (tensors - 1) * bucket + (2 * replicas - 1) * share
         whole(sized(small // 4, 4 * LANES), t_send).wait_send()
@@ -495,6 +515,7 @@
             pltpu.VMEM((groups, SUB, width), F32),
             pltpu.VMEM((max(far, 1), SUB, width), BF16),
             pltpu.VMEM((max(far, 1), SUB, width), BF16),
+            pltpu.VMEM((chips - 1, SUB, width // count), BF16),
             pltpu.VMEM((bucket, rows), BF16),
             pltpu.VMEM((tensors - 1, bucket, rows), BF16),
             pltpu.VMEM((tensors, nch, SUB, tensors * bucket), BF16),
@@ -505,9 +526,9 @@
             pltpu.VMEM((tensors, bucket, wide), BF16),
             pltpu.VMEM((tensors - 1, bucket, wide), BF16),
             dma((5,)), dma((count,)), dma((count + 1,)), dma((chips - 1, nch)),
-            dma((chips - 1, nch + 2)), dma, dma((chips - 1, 4)),
+            dma((chips - 1, 4)), dma, dma((chips - 1, 4)),
             dma, dma, dma, dma((2,)), dma,
-            dma, dma, dma((2,)), dma,
+            dma, dma, dma((2,)), dma, dma, dma,
             pltpu.SemaphoreType.REGULAR((max((replicas // 2 - 1).bit_length(), 1) if reduce_dp else 1,)),
         ],
         compiler_params=pltpu.CompilerParams(

time: 25.3 us -> 25 us (0.988)
  no operation moved by 1% of the time
where the time goes in v8:
time: 25 us; the launch traced here: 24.8 us
  Pallas kernels  24.2 us (97%)
  between operations  0.64 us (3%)
    pallas_call x1, Pallas kernels, body(): pl.pallas_call(functools.partial(kernel, reduce_dp, replicas, tensors), o...  23.1 us
    pallas_call x1, Pallas kernels, store(): pl.pallas_call(functools.partial(store_kernel, count), out_shape=tuple((j...  1.14 us

profile of v8, /device:TPU:0, one launch (start us, length us, event | category | flops | bytes accessed | tf_op | source)
XLA Modules:
  0.0 24.8 jit_solution(7334915481229309237)
XLA Ops:
  0.6 23.1 %shard_map.85 = (f32[32,640]{1,0:T(8,128)S(1)}, bf16[128,384]{1,0:T(8,128)(2,1)S(1)}, bf16[128,5120]{1,0:T(8,128)(2,1)S(1)}) custom-call(bf16[16,8,5120]{2,1,0:T(8,128)(2,1)} %bitcast.9, bf16[4,32,384]{2,1,0:T(8,128)(2,1)} %bitcast.11, bf16[384,5120]{1,0:T(8,128)(2,1)} %w_hbm.1, f32[1,5120]{1,0:T(1,128)} %bitcast.12, bf16[16,8,5120]{2,1,0:T(8,128)(2,1)} %bitcast.10, ...), custom_call_target="tpu_custom_call" | custom-call | tf_op jit(solution)/shard_map/pallas_call | solution.py:494
  23.7 1.1 %shard_map.86 = (f32[32,640]{1,0:T(8,128)}, bf16[128,384]{1,0:T(8,128)(2,1)}, bf16[128,5120]{1,0:T(8,128)(2,1)}) custom-call(f32[32,640]{1,0:T(8,128)S(1)} %get-tuple-element.9.refs_0_, bf16[128,384]{1,0:T(8,128)(2,1)S(1)} %get-tuple-element.10.refs_1_, bf16[128,5120]{1,0:T(8,128)(2,1)S(1)} %get-tuple-element.11.refs_2_), custom_call_target="tpu_custom_call" | custom-call | tf_op jit(solution)/shard_map/pallas_call | solution.py:465

commit v9 on v8

--- a/solution.py
+++ b/solution.py
@@ -195,14 +195,14 @@
             pl.semaphore_wait(barrier, greeted)
         to_mate(j).start()
         if j == 0:
+            for i in others:
+                tell(i).start()
             for i in range(chips - 1):
                 ysend[i * nch, :, span] = own[i * nch, :, span].astype(BF16)
                 across(i, 0, 0, 1).start()
                 unmerged(i).start()
             if reaches:
                 greet(ladder.at[0], 1)
-            for i in others:
-                tell(i).start()
         if j >= LAG:
             merge(j - LAG)
     to_mate(count).start()
@@ -257,7 +257,7 @@
         return pl.ds(pl.multiple_of((owner * nch + k) * SUB, SUB), SUB)
 
     last = nch - 1
-    edges = sorted({0, count * 2 // 5, count * 4 // 5, count})
+    edges = sorted({0, count * 3 // 5, count})
     slices = list(zip(edges, edges[1:]))
 
     def part_of(owner, piece):
@@ -361,9 +361,6 @@
             src_ref=block, dst_ref=block, send_sem=t_send, recv_sem=e_recv,
             device_id={"dp": dp, "tensor": mate}, device_id_type=MESH)
 
-    if reduce_dp:
-        whole(gpick.at[pl.ds(0, replicas - 1), core], d_recv).wait_recv()
-        pass_on().start()
     whole(res, m_recv).wait_recv()
     span = rows_of(chip * 2)
     back = backward(span, 0)
@@ -371,6 +368,8 @@
         back = back + backward(span, j)
     ctx_out[span] = back.astype(BF16)
     if reduce_dp:
+        whole(gpick.at[pl.ds(0, replicas - 1), core], d_recv).wait_recv()
+        pass_on().start()
         whole(gpick.at[pl.ds(0, replicas), 1 - core], e_recv).wait_recv()
         for k in range(nch):
             block = gpick[:, :, k].astype(F32).reshape(half_k, tensors * bucket)

time: 25 us -> 25 us (level)
  no operation moved by 1% of the time
where the time goes in v9:
time: 25 us; the launch traced here: 24.8 us
  Pallas kernels  24.2 us (97%)
  between operations  0.64 us (3%)
    pallas_call x1, Pallas kernels, body(): pl.pallas_call(functools.partial(kernel, reduce_dp, replicas, tensors), o...  23.1 us
    pallas_call x1, Pallas kernels, store(): pl.pallas_call(functools.partial(store_kernel, count), out_shape=tuple((j...  1.14 us

profile of v9, /device:TPU:0, one launch (start us, length us, event | category | flops | bytes accessed | tf_op | source)
XLA Modules:
  0.0 24.8 jit_solution(5403327643150433985)
XLA Ops:
  0.6 23.1 %shard_map.85 = (f32[32,640]{1,0:T(8,128)S(1)}, bf16[128,384]{1,0:T(8,128)(2,1)S(1)}, bf16[128,5120]{1,0:T(8,128)(2,1)S(1)}) custom-call(bf16[16,8,5120]{2,1,0:T(8,128)(2,1)} %bitcast.9, bf16[4,32,384]{2,1,0:T(8,128)(2,1)} %bitcast.11, bf16[384,5120]{1,0:T(8,128)(2,1)} %w_hbm.1, f32[1,5120]{1,0:T(1,128)} %bitcast.12, bf16[16,8,5120]{2,1,0:T(8,128)(2,1)} %bitcast.10, ...), custom_call_target="tpu_custom_call" | custom-call | tf_op jit(solution)/shard_map/pallas_call | solution.py:493
  23.7 1.1 %shard_map.86 = (f32[32,640]{1,0:T(8,128)}, bf16[128,384]{1,0:T(8,128)(2,1)}, bf16[128,5120]{1,0:T(8,128)(2,1)}) custom-call(f32[32,640]{1,0:T(8,128)S(1)} %get-tuple-element.9.refs_0_, bf16[128,384]{1,0:T(8,128)(2,1)S(1)} %get-tuple-element.10.refs_1_, bf16[128,5120]{1,0:T(8,128)(2,1)S(1)} %get-tuple-element.11.refs_2_), custom_call_target="tpu_custom_call" | custom-call | tf_op jit(solution)/shard_map/pallas_call | solution.py:464
